TPU v7x, 128 devices: a whole 4x4x4 slice. The times are simulated.
128 devices in a mesh: dp: 1, ep: 128 (over z, y, x, core).
Axes of the slice: x: 4, y: 4, z: 4, core: 2. Of those that a mesh axis runs over, the one named last changes fastest.
Arguments:
- tokens_a: bfloat16 [16384, 2048], P(('dp', 'ep'))
- experts_a: int32 [16384, 8], P(('dp', 'ep'))
- slots_a: int32 [16384, 8], P(('dp', 'ep'))
- gates_a: bfloat16 [16384, 8], P(('dp', 'ep'))
- tokens_b: bfloat16 [16384, 2048], P(('dp', 'ep'))
- experts_b: int32 [16384, 8], P(('dp', 'ep'))
- slots_b: int32 [16384, 8], P(('dp', 'ep'))
- gates_b: bfloat16 [16384, 8], P(('dp', 'ep'))
- attn_gain: bfloat16 [2048], replicated
- w_query: bfloat16 [2048, 32, 64], replicated
- w_key: bfloat16 [2048, 32, 64], replicated
- w_value: bfloat16 [2048, 32, 64], replicated
- w_out: bfloat16 [32, 64, 2048], replicated
- moe_gain: bfloat16 [2048], replicated
- w_gate: bfloat16 [128, 2048, 768], P('ep')
- w_up: bfloat16 [128, 2048, 768], P('ep')
- w_down: bfloat16 [128, 768, 2048], P('ep')
Outputs:
- output 1: bfloat16 [16384, 2048], P(('dp', 'ep'))
- output 2: bfloat16 [16384, 2048], P(('dp', 'ep'))
All inputs are finite; a program needn't handle non-finite values.
Results may differ from a plain program's by a relative error of at most 0.0156055.
Values are sent between devices in bfloat16 or wider.
A program may use at most 1 GiB of HBM per device.

v0:
```python
import jax
import jax.numpy as jnp
from jax import lax
from jax.experimental import pallas as pl
from jax.experimental.pallas import tpu as pltpu
from jax.sharding import PartitionSpec as P

NORM_EPS = 1e-6
MASK_VALUE = -1e30
RING = 4
CORES = 2
SLOTS = 16
HEAD_DIM = 64
PARTS = (
    (0, 640, ("z", "y", "x")),
    (640, 640, ("x", "z", "y")),
    (1280, 768, ("y", "x", "z")),
)
STRIDE = {"z": 32, "y": 8, "x": 2}

def coords(index):
    return {"z": index // 32, "y": (index // 8) % RING, "x": (index // 2) % RING}, index % CORES


def attention_kernel(xa_ref, xb_ref, ea_ref, sa_ref, ga_ref, eb_ref, sb_ref, gb_ref, attn_gain_ref, moe_gain_ref, wq_ref, wk_ref, wv_ref, wo_ref, res_a_ref, res_b_ref, own_a_ref, own_b_ref, normed_t, total):
    step = pl.program_id(0)
    tokens = xa_ref.shape[0]
    xs = (xa_ref, xb_ref)

    def norm(rows_f, gain_ref):
        inv_rms = lax.rsqrt(jnp.mean(rows_f * rows_f, axis=-1, keepdims=True) + NORM_EPS)
        return rows_f * inv_rms * gain_ref[...].astype(jnp.float32)

    @pl.when(step == 0)
    def _():
        for n, x_ref in enumerate(xs):
            normed_t[:, n * tokens : (n + 1) * tokens] = norm(x_ref[...].astype(jnp.float32), attn_gain_ref).T.astype(jnp.bfloat16)
        total[...] = jnp.zeros_like(total)

    query, keys, values = (jnp.dot(w_ref[...], normed_t[...], preferred_element_type=jnp.float32).astype(jnp.bfloat16) for w_ref in (wq_ref, wk_ref, wv_ref))
    seen = lax.broadcasted_iota(jnp.int32, (tokens, tokens), 0) <= lax.broadcasted_iota(jnp.int32, (tokens, tokens), 1)
    contexts = []
    for n in range(2):
        parts = []
        for start in range(0, query.shape[0], HEAD_DIM):
            rows, cols = slice(start, start + HEAD_DIM), slice(n * tokens, (n + 1) * tokens)
            scores = lax.dot_general(keys[rows, cols], query[rows, cols], (((0,), (0,)), ((), ())), preferred_element_type=jnp.float32) * (HEAD_DIM**-0.5)
            scores = jnp.where(seen, scores, MASK_VALUE)
            weight = jnp.exp(scores - jnp.max(scores, axis=0, keepdims=True))
            prob = (weight / jnp.sum(weight, axis=0, keepdims=True)).astype(jnp.bfloat16)
            parts.append(jnp.dot(values[rows, cols], prob, preferred_element_type=jnp.float32).astype(jnp.bfloat16))
        contexts.append(jnp.concatenate(parts, axis=0))
    context = jnp.concatenate(contexts, axis=1)
    total[...] += lax.dot_general(context, wo_ref[...], (((0,), (0,)), ((), ())), preferred_element_type=jnp.float32)

    @pl.when(step == pl.num_programs(0) - 1)
    def _():
        routing = ((ea_ref, sa_ref, ga_ref), (eb_ref, sb_ref, gb_ref))
        for n, (x_ref, res_ref, own_ref) in enumerate(zip(xs, (res_a_ref, res_b_ref), (own_a_ref, own_b_ref))):
            residual = (x_ref[...].astype(jnp.float32) + total[n * tokens : (n + 1) * tokens, :]).astype(jnp.bfloat16)
            res_ref[...] = residual
            own_ref[0:tokens, :] = norm(residual.astype(jnp.float32), moe_gain_ref).astype(jnp.bfloat16)
            own_ref[tokens : tokens + 8, :] = jnp.zeros((8, own_ref.shape[1]), jnp.bfloat16)
            for start, _, _ in PARTS:
                for i, ref in enumerate(routing[n]):
                    own_ref[tokens : tokens + 8, start + i * 128 : start + (i + 1) * 128] = ref[...].astype(jnp.float32).astype(jnp.bfloat16)


def attention(tokens_a, routing_a, tokens_b, routing_b, attn_gain, moe_gain, w_query, w_key, w_value, w_out):
    tokens, model = tokens_a.shape
    steps = 8
    width = model // steps
    whole = lambda shape: pl.BlockSpec(shape, lambda i: (0,) * len(shape))
    weight = pl.BlockSpec((width, model), lambda i: (i, 0))
    flip = lambda w: jnp.transpose(w, (1, 2, 0)).reshape(model, model)
    rows, choices, gain = (tokens, model), (8, tokens), (1, model)
    own = (tokens + 8, model)
    return pl.pallas_call(
        attention_kernel,
        grid=(steps,),
        out_shape=tuple(jax.ShapeDtypeStruct(shape, jnp.bfloat16) for shape in (rows, rows, own, own)),
        in_specs=[whole(rows)] * 2 + [whole(choices)] * 6 + [whole(gain)] * 2 + [weight] * 4,
        out_specs=(whole(rows), whole(rows), whole(own), whole(own)),
        scratch_shapes=[pltpu.VMEM((model, 2 * tokens), jnp.bfloat16), pltpu.VMEM((2 * tokens, model), jnp.float32)],
        compiler_params=pltpu.CompilerParams(vmem_limit_bytes=40 * 1024 * 1024),
        name="attention",
    )(
        tokens_a, tokens_b, *(r.T for r in routing_a), *(r.T for r in routing_b),
        attn_gain.reshape(gain), moe_gain.reshape(gain), flip(w_query), flip(w_key), flip(w_value), w_out.reshape(model, model),
    )


def row_ids(order):
    s1, s2, s3 = order
    pos, core = coords(lax.axis_index("ep"))
    row = jnp.arange(RING * RING * CORES * SLOTS, dtype=jnp.int32)
    slot = row % SLOTS
    flip = (row // SLOTS) % CORES
    off3 = (row // (SLOTS * CORES)) % RING
    off2 = row // (SLOTS * CORES * RING)
    line = {s1: pos[s1], s2: (pos[s2] + off2) % RING, s3: (pos[s3] + off3) % RING}
    expert = line["z"] * 32 + line["y"] * 8 + line["x"] * 2 + jnp.where(flip == 1, 1 - core, core)
    ids = (expert * SLOTS + slot).astype(jnp.float32)
    return jnp.broadcast_to(ids[:, None], (ids.shape[0], 128))


def peer(dim, delta, flip=0):
    me = lax.axis_index("ep")
    stride = STRIDE[dim]
    place = lax.rem(me // stride, RING)
    other = me + (lax.rem(place + delta % RING, RING) - place) * stride
    if flip:
        other = other + 1 - 2 * lax.rem(me, CORES)
    return {"ep": other}


def send(src, dst, send_sem, recv_sem, where):
    return pltpu.make_async_remote_copy(src_ref=src, dst_ref=dst, send_sem=send_sem, recv_sem=recv_sem, device_id=where, device_id_type=pl.DeviceIdType.MESH)


def drain(ref, sem):
    pltpu.make_async_copy(ref, ref, sem).wait()


def enter():
    barrier = pltpu.get_barrier_semaphore()
    count = 0
    for dim in ("x", "y", "z"):
        for delta in range(1, RING):
            for flip in range(CORES):
                pl.semaphore_signal(barrier, inc=1, device_id=peer(dim, delta, flip), device_id_type=pl.DeviceIdType.MESH)
                count += 1
    pl.semaphore_signal(barrier, inc=1, device_id=peer("x", 0, 1), device_id_type=pl.DeviceIdType.MESH)
    pl.semaphore_wait(barrier, count + 1)


def group_view(rows, part, off3, flip, off2):
    start, width, (_, s2, s3) = PARTS[part]
    place = {s3: off3, s2: off2}
    index = tuple(place.get(dim, slice(None)) for dim in ("y", "z"))
    line = flip * RING + place["x"] if "x" in place else slice(flip * RING, (flip + 1) * RING)
    return rows.at[line, index[0], index[1], :, start : start + width]


PAIRS = tuple((off, flip) for off in range(RING) for flip in range(CORES))


def routing_ids(meta):
    expert = meta[:, 0:128].astype(jnp.float32)
    slot = meta[:, 128:256].astype(jnp.float32)
    return jnp.where(slot >= 0, expert * SLOTS + slot, -1.0)


def dispatch_kernel(ids_ref, *refs):
    batches = 2
    own_refs, out_refs, meta_refs = refs[0:2], refs[2:4], refs[4:6]
    planes = [refs[6 + 3 * n : 9 + 3 * n] for n in range(batches)]
    chosen = [refs[12 + 3 * n : 15 + 3 * n] for n in range(batches)]
    plane_recv, plane_send, row_recv, row_send, local_sem = refs[18:]
    tokens = own_refs[0].shape[0] - 8
    enter()

    def own_part(n, part):
        start, width, _ = PARTS[part]
        return own_refs[n].at[:, start : start + width]

    for n in range(batches):
        for part, (_, _, (s1, s2, _)) in enumerate(PARTS):
            plane = planes[n][part]
            for off in (1, 3, 2):
                send(own_part(n, part), plane.at[off], plane_send.at[n, part], plane_recv.at[n, part, off], peer(s1, off)).start()
                send(own_part(n, part), plane.at[off * RING], plane_send.at[n, part], plane_recv.at[n, part, off * RING], peer(s2, off)).start()

    def forward(n):
        for part, (_, _, (s1, s2, _)) in enumerate(PARTS):
            plane = planes[n][part]
            for off1 in (1, 3, 2):
                drain(plane.at[off1], plane_recv.at[n, part, off1])
                for off2 in (1, 3, 2):
                    send(plane.at[off1], plane.at[off2 * RING + off1], plane_send.at[n, part], plane_recv.at[n, part, off2 * RING + off1], peer(s2, off2)).start()

    def select(n, part, off2, off1, block):
        width = PARTS[part][1]
        ids = ids_ref[part]
        dest = routing_ids(block[tokens : tokens + 8, 0:384])
        hit = ids == dest[0:1, :]
        for j in range(1, 8):
            hit = jnp.logical_or(hit, ids == dest[j : j + 1, :])
        onehot = jnp.where(hit, 1.0, 0.0).astype(jnp.bfloat16)
        rows = jnp.dot(onehot, block[0:tokens, :], preferred_element_type=jnp.float32).astype(jnp.bfloat16)
        chosen[n][part][:, off2, off1] = rows.reshape(8, SLOTS, width)

    def select_group(n, part, off2):
        start, width, _ = PARTS[part]
        plane = planes[n][part]
        if off2 == 0:
            meta_refs[n][part, 0] = own_refs[n][tokens : tokens + 8, start : start + 384]
            for off1 in range(1, RING):
                meta_refs[n][part, off1] = plane[off1, tokens : tokens + 8, 0:384]
            select(n, part, 0, 0, own_refs[n].at[:, start : start + width])
            first = 1
        else:
            for off1 in range(RING):
                drain(plane.at[off2 * RING + off1], plane_recv.at[n, part, off2 * RING + off1])
            first = 0

        def body(off1, carry):
            select(n, part, off2, off1, plane.at[off2 * RING + off1])
            return carry

        lax.fori_loop(first, RING, body, 0)

    def send_group(n, part, off2):
        s3 = PARTS[part][2][2]
        for i in (2, 3, 6, 7, 4, 5, 1):
            off3, flip = PAIRS[i]
            send(chosen[n][part].at[i, off2], group_view(out_refs[n], part, off3, flip, off2), row_send.at[n, part], row_recv.at[n], peer(s3, off3, flip)).start()
        pltpu.make_async_copy(chosen[n][part].at[0, off2], group_view(out_refs[n], part, 0, 0, off2), local_sem.at[n, part]).start()

    forward(0)
    for n in range(batches):
        late = None
        for off2 in (0, 1, 3, 2):
            for part in range(3):
                select_group(n, part, off2)
                if late is not None:
                    send_group(*late)
                late = (n, part, off2)
            if n == 0 and off2 == 0:
                forward(1)
        send_group(*late)

    for n in range(batches):
        drain(out_refs[n].at[1:8], row_recv.at[n])
        for part in range(3):
            plane = planes[n][part]
            drain(plane.at[1:16], plane_send.at[n, part])
            drain(chosen[n][part].at[1:8], row_send.at[n, part])
            drain(chosen[n][part].at[0], local_sem.at[n, part])


def dispatch(own_a, own_b, ids):
    rows, model = own_a.shape
    out = jax.ShapeDtypeStruct((CORES * RING, RING, RING, SLOTS, model), jnp.bfloat16)
    meta = jax.ShapeDtypeStruct((3, RING, 8, 384), jnp.bfloat16)
    any_spec, vmem_spec = pl.BlockSpec(memory_space=pl.ANY), pl.BlockSpec(memory_space=pltpu.VMEM)
    plane = [pltpu.VMEM((RING * RING, rows, width), jnp.bfloat16) for _, width, _ in PARTS]
    chosen = [pltpu.VMEM((8, RING, RING, SLOTS, width), jnp.bfloat16) for _, width, _ in PARTS]
    dma = pltpu.SemaphoreType.DMA
    return pl.pallas_call(
        dispatch_kernel,
        out_shape=(out, out, meta, meta),
        in_specs=[vmem_spec] * 3,
        out_specs=(any_spec, any_spec, vmem_spec, vmem_spec),
        scratch_shapes=plane * 2 + chosen * 2 + [dma((2, 3, 16)), dma((2, 3)), dma((2,)), dma((2, 3)), dma((2, 3))],
        compiler_params=pltpu.CompilerParams(collective_id=0, has_side_effects=True, vmem_limit_bytes=56 * 1024 * 1024),
        name="dispatch_rows",
    )(ids, own_a, own_b)


def return_kernel(ids_ref, *refs):
    batches = 2
    out_refs, meta_refs, res_refs, y_refs = refs[0:2], refs[2:4], refs[4:6], refs[6:8]
    scratch = refs[8:]
    back = [scratch[0 + 3 * n : 3 + 3 * n] for n in range(batches)]
    rows = [scratch[6 + 3 * n : 9 + 3 * n] for n in range(batches)]
    sums = [scratch[12 + 3 * n : 15 + 3 * n] for n in range(batches)]
    got = [scratch[18 + 3 * n : 21 + 3 * n] for n in range(batches)]
    back_recv, back_send, own_sem, rows_recv, rows_send, sums_recv, sums_send = scratch[24:]
    tokens = y_refs[0].shape[0]
    enter()

    for n in range(batches):
        for part in range(3):
            for off2 in range(RING):
                pltpu.make_async_copy(group_view(out_refs[n], part, 0, 0, off2), back[n][part].at[0, off2], own_sem.at[n, part]).start()
        for off2 in (2, 1, 3, 0):
            for i in (2, 3, 6, 7, 4, 5, 1):
                off3, flip = PAIRS[i]
                for part in range(3):
                    s3 = PARTS[part][2][2]
                    send(group_view(out_refs[n], part, off3, flip, off2), back[n][part].at[i, off2], back_send.at[n, part], back_recv.at[n, part, off2], peer(s3, -off3, flip)).start()

    def turn(n, off2):
        for part in range(3):
            s2 = PARTS[part][2][1]
            drain(back[n][part].at[1:8, off2], back_recv.at[n, part, off2])
            if off2:
                send(back[n][part].at[:, off2], rows[n][part].at[off2 - 1], rows_send.at[n, part], rows_recv.at[n, part, off2 - 1], peer(s2, -off2)).start()

    def weighted(n, part, off1):
        width = PARTS[part][1]
        meta = meta_refs[n][part, off1]
        dest = routing_ids(meta)
        gates = meta[:, 256:384].astype(jnp.float32)
        total = None
        for off2 in range(RING):
            ids = ids_ref[part, off2 * 128 : (off2 + 1) * 128, :]
            weight = jnp.zeros((128, tokens), jnp.float32)
            for j in range(8):
                weight = jnp.where(ids == dest[j : j + 1, :], gates[j : j + 1, :], weight)
            block = back[n][part][:, 0, off1] if off2 == 0 else rows[n][part][off2 - 1, :, off1]
            term = lax.dot_general(weight.astype(jnp.bfloat16), block.reshape(128, width), (((0,), (0,)), ((), ())), preferred_element_type=jnp.float32)
            total = term if total is None else total + term
        return total

    def own_ready(n):
        for part in range(3):
            drain(back[n][part].at[0], own_sem.at[n, part])

    def combine(n):
        for part in range(3):
            start, width, (s1, _, _) = PARTS[part]
            for off2 in (1, 3, 2):
                drain(rows[n][part].at[off2 - 1], rows_recv.at[n, part, off2 - 1])
            for off1 in (2, 1, 3):
                sums[n][part][off1 - 1] = weighted(n, part, off1)
            y_refs[n][:, start : start + width] = res_refs[n][:, start : start + width].astype(jnp.float32) + weighted(n, part, 0)
            for off1 in (2, 1, 3):
                send(sums[n][part].at[off1 - 1], got[n][part].at[off1 - 1], sums_send.at[n, part], sums_recv.at[n, part, off1 - 1], peer(s1, -off1)).start()

    def finish(n):
        for part in range(3):
            start, width, _ = PARTS[part]
            total = y_refs[n][:, start : start + width]
            for off1 in range(1, RING):
                drain(got[n][part].at[off1 - 1], sums_recv.at[n, part, off1 - 1])
                total = total + got[n][part][off1 - 1]
            y_refs[n][:, start : start + width] = total

    own_ready(0)
    for off2 in (2, 1, 3, 0):
        turn(0, off2)
    own_ready(1)
    turn(1, 2)
    combine(0)
    for off2 in (1, 3, 0):
        turn(1, off2)
    finish(0)
    combine(1)
    finish(1)
    for n in range(batches):
        for part in range(3):
            drain(back[n][part].at[1:8], back_send.at[n, part])
            drain(rows[n][part], rows_send.at[n, part])
            drain(sums[n][part], sums_send.at[n, part])


def bring_back(ids, outs, metas, residuals):
    tokens, model = residuals[0].shape
    y = jax.ShapeDtypeStruct((tokens, model), jnp.float32)
    any_spec, vmem_spec = pl.BlockSpec(memory_space=pl.ANY), pl.BlockSpec(memory_space=pltpu.VMEM)
    widths = [width for _, width, _ in PARTS]
    back = [pltpu.VMEM((8, RING, RING, SLOTS, width), jnp.bfloat16) for width in widths]
    rows = [pltpu.VMEM((RING - 1, 8, RING, SLOTS, width), jnp.bfloat16) for width in widths]
    sums = [pltpu.VMEM((RING - 1, tokens, width), jnp.float32) for width in widths]
    dma = pltpu.SemaphoreType.DMA
    return pl.pallas_call(
        return_kernel,
        out_shape=(y, y),
        in_specs=[vmem_spec] + [any_spec] * 2 + [vmem_spec] * 4,
        out_specs=(vmem_spec, vmem_spec),
        scratch_shapes=back * 2 + rows * 2 + sums * 2 + sums * 2
        + [dma((2, 3, RING)), dma((2, 3)), dma((2, 3)), dma((2, 3, 3)), dma((2, 3)), dma((2, 3, 3)), dma((2, 3))],
        compiler_params=pltpu.CompilerParams(collective_id=1, has_side_effects=True, vmem_limit_bytes=60 * 1024 * 1024),
        name="return_rows",
    )(ids, *outs, *metas, *residuals)


def ffn_kernel(x_ref, wg_ref, wu_ref, wd_ref, o_ref):
    x = x_ref[...].reshape(-1, wg_ref.shape[0])
    gate_act = jnp.dot(x, wg_ref[...], preferred_element_type=jnp.float32)
    up_act = jnp.dot(x, wu_ref[...], preferred_element_type=jnp.float32)
    hidden = (jax.nn.silu(gate_act) * up_act).astype(jnp.bfloat16)
    o_ref[...] = jnp.dot(hidden, wd_ref[...], preferred_element_type=jnp.float32).astype(jnp.bfloat16).reshape(o_ref.shape)


def expert_ffn(x, w_gate, w_up, w_down):
    model, ffn = w_gate.shape
    block = pl.BlockSpec((1,) + x.shape[1:], lambda i: (i, 0, 0, 0, 0))
    return pl.pallas_call(
        ffn_kernel,
        grid=(RING * CORES,),
        out_shape=jax.ShapeDtypeStruct(x.shape, x.dtype),
        in_specs=[block, pl.BlockSpec((model, ffn), lambda i: (0, 0)), pl.BlockSpec((model, ffn), lambda i: (0, 0)), pl.BlockSpec((ffn, model), lambda i: (0, 0))],
        out_specs=block,
        compiler_params=pltpu.CompilerParams(vmem_limit_bytes=40 * 1024 * 1024),
        cost_estimate=pl.CostEstimate(flops=6 * 2048 * model * ffn, bytes_accessed=26 * 1024 * 1024, transcendentals=2048 * ffn),
        name="expert_ffn",
    )(x, w_gate, w_up, w_down)


def solution(mesh):
    row_spec = P(("dp", "ep"), None)
    full_spec = P(None, None, None)
    gain_spec = P(None)
    expert_spec = P("ep", None, None)
    in_specs = (row_spec,) * 8 + (gain_spec,) + (full_spec,) * 4 + (gain_spec,) + (expert_spec,) * 3

    def device_fn(tokens_a, experts_a, slots_a, gates_a, tokens_b, experts_b, slots_b, gates_b, attn_gain, w_query, w_key, w_value, w_out, moe_gain, w_gate, w_up, w_down):
        w_gate, w_up, w_down = w_gate[0], w_up[0], w_down[0]
        ids = jnp.stack([row_ids(order) for _, _, order in PARTS])

        res_a, res_b, own_a, own_b = attention(
            tokens_a, (experts_a, slots_a, gates_a), tokens_b, (experts_b, slots_b, gates_b), attn_gain, moe_gain, w_query, w_key, w_value, w_out
        )
        x_a, x_b, meta_a, meta_b = dispatch(own_a, own_b, ids[:, :128])
        o_a = expert_ffn(x_a, w_gate, w_up, w_down)
        o_b = expert_ffn(x_b, w_gate, w_up, w_down)
        y_a, y_b = bring_back(ids, (o_a, o_b), (meta_a, meta_b), (res_a, res_b))
        return y_a.astype(jnp.bfloat16), y_b.astype(jnp.bfloat16)

    return jax.shard_map(device_fn, mesh=mesh, in_specs=in_specs, out_specs=(row_spec, row_spec), check_vma=False)
```

profile of v0, /device:TPU:0, one launch (start us, length us, event | category | flops | bytes accessed | tf_op | source)
XLA Modules:
  0.0 420.6 jit_solution(7882146833611671174)
XLA Ops:
  0.8 0.7 reshape.22.attn_gain_ref
  1.5 0.7 reshape.23.moe_gain_ref
  2.1 0.1 stack_broadcast_in_dim.6
  2.3 0.1 stack_broadcast_in_dim.8
  2.4 0.1 stack_broadcast_in_dim.7
  2.5 0.1 pad_maximum_fusion.ids_ref
  2.6 0.0 copy-start.16
  2.6 0.8 slice.4.ids_ref
  3.4 0.0 copy-start
  3.4 3.4 copy-done
  6.8 0.0 copy-start.3
  6.8 1.0 copy-done.3
  7.8 0.0 copy-start.4
  7.8 1.0 copy-done.4
  8.8 0.0 copy-start.7
  8.8 0.7 copy-done.7
  9.5 0.0 copy-start.8
  9.5 0.7 copy-done.8
  10.2 0.0 copy-start.9
  10.2 0.7 copy-done.9
  10.9 0.0 copy-start.10
  10.9 0.7 copy-done.10
  11.6 0.0 copy-start.11
  11.6 0.7 copy-done.11
  12.3 0.0 copy-start.12
  12.3 0.7 copy-done.12
  13.0 0.0 copy-start.13
  13.0 0.0 copy-start.14
  13.0 29.9 %attention.1 = (bf16[128,2048]{1,0:T(8,128)(2,1)S(1)}, bf16[128,2048]{1,0:T(8,128)(2,1)S(1)}, bf16[136,2048]{1,0:T(8,128)(2,1)S(1)}, bf16[136,2048]{1,0:T(8,128)(2,1)S(1)}) custom-call(bf16[128,2048]{1,0:T(8,128)(2,1)S(1)} %copy-done.3, bf16[128,2048]{1,0:T(8,128)(2,1)S(1)} %copy-done.4, s32[8,128]{1,0:T(8,128)S(1)} %bitcast.20, s32[8,128]{1,0:T(8,128)S(1)} %bitcast.21, ...), custom_call_target="tpu_custom_call" | custom-call | tf_op jit(solution)/shard_map/attention/pallas_call | solution.py:78
  42.9 0.0 copy-done.16
  42.9 0.0 copy-start.1
  42.9 0.9 copy-done.1
  43.8 0.0 copy-start.2
  43.8 0.8 copy-done.2
  44.6 0.0 copy-start.5
  44.6 0.8 copy-done.5
  45.4 0.0 copy-start.6
  45.4 0.8 copy-done.6
  46.2 153.4 %dispatch_rows.1 = (bf16[8,4,4,16,2048]{4,3,2,1,0:T(8,128)(2,1)}, bf16[8,4,4,16,2048]{4,3,2,1,0:T(8,128)(2,1)}, bf16[3,4,8,384]{3,2,1,0:T(8,128)(2,1)}, bf16[3,4,8,384]{3,2,1,0:T(8,128)(2,1)}) custom-call(f32[3,128,128]{2,1,0:T(8,128)} %slice.4.ids_ref, bf16[136,2048]{1,0:T(8,128)(2,1)} %copy-done.1, bf16[136,2048]{1,0:T(8,128)(2,1)} %copy-done.2), custom_call_target="tpu_custom_call" | custom-call | tf_op jit(solution)/shard_map/dispatch_rows/pallas_call | solution.py:250
  199.6 0.0 copy-done.13
  199.6 0.0 copy-done.14
  199.7 0.0 copy-start.15
  199.7 1.9 copy-done.15
  201.5 23.2 %expert_ffn.2.refs_0_ = bf16[8,4,4,16,2048]{4,3,2,1,0:T(8,128)(2,1)} custom-call(bf16[8,4,4,16,2048]{4,3,2,1,0:T(8,128)(2,1)} %get-tuple-element.14.x_ref, bf16[2048,768]{1,0:T(8,128)(2,1)S(1)} %bitcast.26, bf16[2048,768]{1,0:T(8,128)(2,1)S(1)} %bitcast.28, bf16[768,2048]{1,0:T(8,128)(2,1)S(1)} %bitcast.30), custom_call_target="tpu_custom_call" | custom-call | flops 19327352832 | bytes 27262976 | tf_op jit(solution)/shard_map/expert_ffn/pallas_call | solution.py:381
  224.7 23.3 %expert_ffn.3.refs_1_ = bf16[8,4,4,16,2048]{4,3,2,1,0:T(8,128)(2,1)} custom-call(bf16[8,4,4,16,2048]{4,3,2,1,0:T(8,128)(2,1)} %get-tuple-element.15.x_ref, bf16[2048,768]{1,0:T(8,128)(2,1)S(1)} %bitcast.27, bf16[2048,768]{1,0:T(8,128)(2,1)S(1)} %bitcast.29, bf16[768,2048]{1,0:T(8,128)(2,1)S(1)} %bitcast.31), custom_call_target="tpu_custom_call" | custom-call | flops 19327352832 | bytes 27262976 | tf_op jit(solution)/shard_map/expert_ffn/pallas_call | solution.py:381
  248.0 168.4 %return_rows.1 = (f32[128,2048]{1,0:T(8,128)}, f32[128,2048]{1,0:T(8,128)}) custom-call(f32[3,512,128]{2,1,0:T(8,128)} %copy-done.16, bf16[8,4,4,16,2048]{4,3,2,1,0:T(8,128)(2,1)} %expert_ffn.2.refs_0_, bf16[8,4,4,16,2048]{4,3,2,1,0:T(8,128)(2,1)} %expert_ffn.3.refs_1_, bf16[3,4,8,384]{3,2,1,0:T(8,128)(2,1)} %get-tuple-element.16.refs_2_, ...), custom_call_target="tpu_custom_call" | custom-call | tf_op jit(solution)/shard_map/return_rows/pallas_call | solution.py:358
  416.4 2.1 convert_element_type.18
  418.5 2.1 convert_element_type.19
  (2 shorter events, 0.1 us)
Async XLA Ops:
  2.6 40.3 %copy-start.16 = (f32[3,512,128]{2,1,0:T(8,128)}, f32[3,512,128]{2,1,0:T(8,128)S(1)}, u32[]{:S(2)}) copy-start(f32[3,512,128]{2,1,0:T(8,128)S(1)} %pad_maximum_fusion.ids_ref) | copy-start | bytes 2359300
  3.4 3.4 copy-start
  6.8 1.0 copy-start.3
  7.8 1.0 copy-start.4
  8.8 0.7 copy-start.7
  9.5 0.7 copy-start.8
  10.2 0.7 copy-start.9
  10.9 0.7 copy-start.10
  11.6 0.7 copy-start.11
  12.3 0.7 copy-start.12
  13.0 186.7 %copy-start.13 = (bf16[1,2048,768]{2,1,0:T(8,128)(2,1)S(1)}, bf16[1,2048,768]{2,1,0:T(8,128)(2,1)}, u32[]{:S(2)}) copy-start(bf16[1,2048,768]{2,1,0:T(8,128)(2,1)} %param.31) | copy-start | bytes 9437188
  13.0 186.7 %copy-start.14 = (bf16[1,2048,768]{2,1,0:T(8,128)(2,1)S(1)}, bf16[1,2048,768]{2,1,0:T(8,128)(2,1)}, u32[]{:S(2)}) copy-start(bf16[1,2048,768]{2,1,0:T(8,128)(2,1)} %param.32) | copy-start | bytes 9437188
  42.9 0.9 copy-start.1
  43.8 0.8 copy-start.2
  44.6 0.8 copy-start.5
  45.4 0.8 copy-start.6
  199.7 1.9 copy-start.15
where the time goes:
time: 421 us
  Pallas kernels  398 us (95%)
  local copies, waits for them, and re-layouts  17.3 us (4%)
  other arithmetic  4.27 us (1%)
    pallas_call x1, Pallas kernels, bring_back(): pl.pallas_call(return_kernel, out_shape=(y, y), in_specs=[vmem_spec] + [a...  168 us
    pallas_call x1, Pallas kernels, dispatch(): pl.pallas_call(dispatch_kernel, out_shape=(out, out, meta, meta), in_spec...  153 us
    pallas_call x2, Pallas kernels, expert_ffn(): pl.pallas_call(ffn_kernel, grid=(RING * CORES,), out_shape=jax.ShapeDtype...  46.4 us
    pallas_call x1, Pallas kernels, attention(): pl.pallas_call(attention_kernel, grid=(steps,), out_shape=tuple((jax.Shap...  29.9 us
    unnamed x34, local copies, waits for them, and re-layouts  14.7 us

commit v1 on v0

--- a/solution.py
+++ b/solution.py
@@ -29,7 +29,7 @@
 
     def norm(rows_f, gain_ref):
         inv_rms = lax.rsqrt(jnp.mean(rows_f * rows_f, axis=-1, keepdims=True) + NORM_EPS)
-        return rows_f * inv_rms * gain_ref[...].astype(jnp.float32)
+        return rows_f * inv_rms * gain_ref[...].astype(jnp.float32).reshape(1, -1)
 
     @pl.when(step == 0)
     def _():
@@ -73,7 +73,7 @@
     whole = lambda shape: pl.BlockSpec(shape, lambda i: (0,) * len(shape))
     weight = pl.BlockSpec((width, model), lambda i: (i, 0))
     flip = lambda w: jnp.transpose(w, (1, 2, 0)).reshape(model, model)
-    rows, choices, gain = (tokens, model), (8, tokens), (1, model)
+    rows, choices, gain = (tokens, model), (8, tokens), (model,)
     own = (tokens + 8, model)
     return pl.pallas_call(
         attention_kernel,
@@ -82,11 +82,11 @@
         in_specs=[whole(rows)] * 2 + [whole(choices)] * 6 + [whole(gain)] * 2 + [weight] * 4,
         out_specs=(whole(rows), whole(rows), whole(own), whole(own)),
         scratch_shapes=[pltpu.VMEM((model, 2 * tokens), jnp.bfloat16), pltpu.VMEM((2 * tokens, model), jnp.float32)],
-        compiler_params=pltpu.CompilerParams(vmem_limit_bytes=40 * 1024 * 1024),
+        compiler_params=pltpu.CompilerParams(vmem_limit_bytes=62 * 1024 * 1024),
         name="attention",
     )(
         tokens_a, tokens_b, *(r.T for r in routing_a), *(r.T for r in routing_b),
-        attn_gain.reshape(gain), moe_gain.reshape(gain), flip(w_query), flip(w_key), flip(w_value), w_out.reshape(model, model),
+        attn_gain, moe_gain, flip(w_query), flip(w_key), flip(w_value), w_out.reshape(model, model),
     )
 
 
@@ -151,14 +151,76 @@
     return jnp.where(slot >= 0, expert * SLOTS + slot, -1.0)
 
 
+def load_weights(w_refs, held, sem):
+    copies = [pltpu.make_async_copy(src, dst, sem.at[i]) for i, (src, dst) in enumerate(zip(w_refs, held))]
+    for copy in copies:
+        copy.start()
+    return copies
+
+
+def run_experts(x_ref, o_ref, held, x_buf, o_buf, x_sem, o_sem, between):
+    blocks = x_ref.shape[0]
+    gate_w, up_w, down_w = held
+
+    def load(b, slot):
+        return pltpu.make_async_copy(x_ref.at[b], x_buf.at[slot], x_sem.at[slot])
+
+    load(0, 0).start()
+
+    def step(b, carry):
+        slot = lax.rem(b, 2)
+
+        @pl.when(b + 1 < blocks)
+        def _():
+            load(b + 1, 1 - slot).start()
+
+        load(b, slot).wait()
+
+        @pl.when(b >= 2)
+        def _():
+            drain(o_buf.at[slot], o_sem.at[slot])
+
+        x = x_buf[slot].reshape(-1, gate_w.shape[0])
+        gate_act = jnp.dot(x, gate_w[...], preferred_element_type=jnp.float32)
+        up_act = jnp.dot(x, up_w[...], preferred_element_type=jnp.float32)
+        hidden = (jax.nn.silu(gate_act) * up_act).astype(jnp.bfloat16)
+        o_buf[slot] = jnp.dot(hidden, down_w[...], preferred_element_type=jnp.float32).astype(jnp.bfloat16).reshape(o_buf.shape[1:])
+        pltpu.make_async_copy(o_buf.at[slot], o_ref.at[b], o_sem.at[slot]).start()
+        between(b)
+        return carry
+
+    lax.fori_loop(0, blocks, step, 0)
+    for slot in range(2):
+        drain(o_buf.at[slot], o_sem.at[slot])
+
+
+def expert_scratch(model, ffn):
+    block = (2, RING, RING, SLOTS, model)
+    dma = pltpu.SemaphoreType.DMA
+    return [
+        pltpu.VMEM((model, ffn), jnp.bfloat16),
+        pltpu.VMEM((model, ffn), jnp.bfloat16),
+        pltpu.VMEM((ffn, model), jnp.bfloat16),
+        pltpu.VMEM(block, jnp.bfloat16),
+        pltpu.VMEM(block, jnp.bfloat16),
+        dma((3,)),
+        dma((2,)),
+        dma((2,)),
+    ]
+
+
 def dispatch_kernel(ids_ref, *refs):
     batches = 2
-    own_refs, out_refs, meta_refs = refs[0:2], refs[2:4], refs[4:6]
-    planes = [refs[6 + 3 * n : 9 + 3 * n] for n in range(batches)]
-    chosen = [refs[12 + 3 * n : 15 + 3 * n] for n in range(batches)]
-    plane_recv, plane_send, row_recv, row_send, local_sem = refs[18:]
+    own_refs, w_refs, out_refs, meta_refs, done_ref = refs[0:2], refs[2:5], refs[5:7], refs[7:9], refs[9]
+    scratch = refs[10:]
+    planes = [scratch[3 * n : 3 + 3 * n] for n in range(batches)]
+    chosen = [scratch[6 + 3 * n : 9 + 3 * n] for n in range(batches)]
+    plane_recv, plane_send, row_recv, row_send, local_sem = scratch[12:17]
+    held, (x_buf, o_buf, w_sem, x_sem, o_sem) = scratch[17:20], scratch[20:]
     tokens = own_refs[0].shape[0] - 8
+    half = tokens // 2
     enter()
+    weight_copies = load_weights(w_refs, held, w_sem)
 
     def own_part(n, part):
         start, width, _ = PARTS[part]
@@ -169,6 +231,7 @@
             plane = planes[n][part]
             for off in (1, 3, 2):
                 send(own_part(n, part), plane.at[off], plane_send.at[n, part], plane_recv.at[n, part, off], peer(s1, off)).start()
+            for off in (1, 3):
                 send(own_part(n, part), plane.at[off * RING], plane_send.at[n, part], plane_recv.at[n, part, off * RING], peer(s2, off)).start()
 
     def forward(n):
@@ -176,8 +239,16 @@
             plane = planes[n][part]
             for off1 in (1, 3, 2):
                 drain(plane.at[off1], plane_recv.at[n, part, off1])
-                for off2 in (1, 3, 2):
+                for off2 in (1, 3):
                     send(plane.at[off1], plane.at[off2 * RING + off1], plane_send.at[n, part], plane_recv.at[n, part, off2 * RING + off1], peer(s2, off2)).start()
+
+    def relay(n, off2):
+        rows = slice(0, half) if off2 == 1 else slice(half, tokens + 8)
+        for part, (_, _, (s1, s2, _)) in enumerate(PARTS):
+            plane = planes[n][part]
+            for off1 in range(RING):
+                drain(plane.at[off2 * RING + off1], plane_recv.at[n, part, off2 * RING + off1])
+                send(plane.at[off2 * RING + off1, rows], plane.at[2 * RING + off1, rows], plane_send.at[n, part], plane_recv.at[n, part, 2 * RING + off1], peer(s2, off2)).start()
 
     def select(n, part, off2, off1, block):
         width = PARTS[part][1]
@@ -200,7 +271,7 @@
             select(n, part, 0, 0, own_refs[n].at[:, start : start + width])
             first = 1
         else:
-            for off1 in range(RING):
+            for off1 in range(RING if off2 == 2 else 0):
                 drain(plane.at[off2 * RING + off1], plane_recv.at[n, part, off2 * RING + off1])
             first = 0
 
@@ -217,30 +288,48 @@
             send(chosen[n][part].at[i, off2], group_view(out_refs[n], part, off3, flip, off2), row_send.at[n, part], row_recv.at[n], peer(s3, off3, flip)).start()
         pltpu.make_async_copy(chosen[n][part].at[0, off2], group_view(out_refs[n], part, 0, 0, off2), local_sem.at[n, part]).start()
 
+    late = []
+
+    def groups(n, off2):
+        for part in range(3):
+            select_group(n, part, off2)
+            if late:
+                send_group(*late.pop())
+            late.append((n, part, off2))
+
     forward(0)
+    groups(0, 0)
+    forward(1)
+    relay(0, 1)
+    relay(0, 3)
+    groups(0, 1)
+    groups(0, 3)
+    relay(1, 1)
+    relay(1, 3)
+    groups(0, 2)
+    for off2 in (0, 1, 3, 2):
+        groups(1, off2)
+    send_group(*late.pop())
+
+    def rows_done(n):
+        drain(out_refs[n].at[1:8], row_recv.at[n])
+        for part in range(3):
+            drain(chosen[n][part].at[0], local_sem.at[n, part])
+
+    rows_done(0)
+    for copy in weight_copies:
+        copy.wait()
+    run_experts(out_refs[0], done_ref, held, x_buf, o_buf, x_sem, o_sem, lambda b: None)
+    rows_done(1)
     for n in range(batches):
-        late = None
-        for off2 in (0, 1, 3, 2):
-            for part in range(3):
-                select_group(n, part, off2)
-                if late is not None:
-                    send_group(*late)
-                late = (n, part, off2)
-            if n == 0 and off2 == 0:
-                forward(1)
-        send_group(*late)
-
-    for n in range(batches):
-        drain(out_refs[n].at[1:8], row_recv.at[n])
-        for part in range(3):
-            plane = planes[n][part]
-            drain(plane.at[1:16], plane_send.at[n, part])
+        for part in range(3):
+            drain(planes[n][part].at[1:16], plane_send.at[n, part])
             drain(chosen[n][part].at[1:8], row_send.at[n, part])
-            drain(chosen[n][part].at[0], local_sem.at[n, part])
-
-
-def dispatch(own_a, own_b, ids):
+
+
+def dispatch(own_a, own_b, ids, weights):
     rows, model = own_a.shape
+    ffn = weights[0].shape[1]
     out = jax.ShapeDtypeStruct((CORES * RING, RING, RING, SLOTS, model), jnp.bfloat16)
     meta = jax.ShapeDtypeStruct((3, RING, 8, 384), jnp.bfloat16)
     any_spec, vmem_spec = pl.BlockSpec(memory_space=pl.ANY), pl.BlockSpec(memory_space=pltpu.VMEM)
@@ -249,28 +338,31 @@
     dma = pltpu.SemaphoreType.DMA
     return pl.pallas_call(
         dispatch_kernel,
-        out_shape=(out, out, meta, meta),
-        in_specs=[vmem_spec] * 3,
-        out_specs=(any_spec, any_spec, vmem_spec, vmem_spec),
-        scratch_shapes=plane * 2 + chosen * 2 + [dma((2, 3, 16)), dma((2, 3)), dma((2,)), dma((2, 3)), dma((2, 3))],
-        compiler_params=pltpu.CompilerParams(collective_id=0, has_side_effects=True, vmem_limit_bytes=56 * 1024 * 1024),
+        out_shape=(out, out, meta, meta, out),
+        in_specs=[vmem_spec] * 3 + [any_spec] * 3,
+        out_specs=(any_spec, any_spec, vmem_spec, vmem_spec, any_spec),
+        scratch_shapes=plane * 2 + chosen * 2 + [dma((2, 3, 16)), dma((2, 3)), dma((2,)), dma((2, 3)), dma((2, 3))] + expert_scratch(model, ffn),
+        compiler_params=pltpu.CompilerParams(collective_id=0, has_side_effects=True, vmem_limit_bytes=62 * 1024 * 1024),
         name="dispatch_rows",
-    )(ids, own_a, own_b)
+    )(ids, own_a, own_b, *weights)
 
 
 def return_kernel(ids_ref, *refs):
     batches = 2
-    out_refs, meta_refs, res_refs, y_refs = refs[0:2], refs[2:4], refs[4:6], refs[6:8]
-    scratch = refs[8:]
+    done_a, x_b, meta_refs, res_refs, w_refs = refs[0], refs[1], refs[2:4], refs[4:6], refs[6:9]
+    y_refs, done_b, scratch = refs[9:11], refs[11], refs[12:]
+    out_refs = (done_a, done_b)
     back = [scratch[0 + 3 * n : 3 + 3 * n] for n in range(batches)]
     rows = [scratch[6 + 3 * n : 9 + 3 * n] for n in range(batches)]
-    sums = [scratch[12 + 3 * n : 15 + 3 * n] for n in range(batches)]
-    got = [scratch[18 + 3 * n : 21 + 3 * n] for n in range(batches)]
-    back_recv, back_send, own_sem, rows_recv, rows_send, sums_recv, sums_send = scratch[24:]
+    sums, got = scratch[12:15], [scratch[15 + 3 * n : 18 + 3 * n] for n in range(batches)]
+    kept = scratch[21]
+    back_recv, back_send, own_sem, rows_recv, rows_send, sums_recv, sums_send = scratch[22:29]
+    held, (x_buf, o_buf, w_sem, x_sem, o_sem) = scratch[29:32], scratch[32:]
     tokens = y_refs[0].shape[0]
     enter()
-
-    for n in range(batches):
+    weight_copies = load_weights(w_refs, held, w_sem)
+
+    def hand_out(n):
         for part in range(3):
             for off2 in range(RING):
                 pltpu.make_async_copy(group_view(out_refs[n], part, 0, 0, off2), back[n][part].at[0, off2], own_sem.at[n, part]).start()
@@ -314,27 +406,39 @@
             for off2 in (1, 3, 2):
                 drain(rows[n][part].at[off2 - 1], rows_recv.at[n, part, off2 - 1])
             for off1 in (2, 1, 3):
-                sums[n][part][off1 - 1] = weighted(n, part, off1)
-            y_refs[n][:, start : start + width] = res_refs[n][:, start : start + width].astype(jnp.float32) + weighted(n, part, 0)
+                sums[part][off1 - 1] = weighted(n, part, off1)
+            kept[:, start : start + width] = res_refs[n][:, start : start + width].astype(jnp.float32) + weighted(n, part, 0)
             for off1 in (2, 1, 3):
-                send(sums[n][part].at[off1 - 1], got[n][part].at[off1 - 1], sums_send.at[n, part], sums_recv.at[n, part, off1 - 1], peer(s1, -off1)).start()
+                send(sums[part].at[off1 - 1], got[n][part].at[off1 - 1], sums_send.at[part], sums_recv.at[n, part, off1 - 1], peer(s1, -off1)).start()
 
     def finish(n):
         for part in range(3):
             start, width, _ = PARTS[part]
-            total = y_refs[n][:, start : start + width]
+            total = kept[:, start : start + width]
             for off1 in range(1, RING):
                 drain(got[n][part].at[off1 - 1], sums_recv.at[n, part, off1 - 1])
                 total = total + got[n][part][off1 - 1]
-            y_refs[n][:, start : start + width] = total
-
-    own_ready(0)
+            y_refs[n][:, start : start + width] = total.astype(y_refs[n].dtype)
+            drain(sums[part], sums_send.at[part])
+
+    hand_out(0)
+    for copy in weight_copies:
+        copy.wait()
+
+    def between(b):
+        for when, off2 in ((1, 2), (3, 1), (5, 3), (7, 0)):
+
+            @pl.when(b == when)
+            def _():
+                if off2 == 2:
+                    own_ready(0)
+                turn(0, off2)
+
+    run_experts(x_b, done_b, held, x_buf, o_buf, x_sem, o_sem, between)
+    hand_out(1)
+    combine(0)
+    own_ready(1)
     for off2 in (2, 1, 3, 0):
-        turn(0, off2)
-    own_ready(1)
-    turn(1, 2)
-    combine(0)
-    for off2 in (1, 3, 0):
         turn(1, off2)
     finish(0)
     combine(1)
@@ -343,12 +447,12 @@
         for part in range(3):
             drain(back[n][part].at[1:8], back_send.at[n, part])
             drain(rows[n][part], rows_send.at[n, part])
-            drain(sums[n][part], sums_send.at[n, part])
-
-
-def bring_back(ids, outs, metas, residuals):
+
+
+def bring_back(ids, done_a, x_b, metas, residuals, weights):
     tokens, model = residuals[0].shape
-    y = jax.ShapeDtypeStruct((tokens, model), jnp.float32)
+    ffn = weights[0].shape[1]
+    y = jax.ShapeDtypeStruct((tokens, model), jnp.bfloat16)
     any_spec, vmem_spec = pl.BlockSpec(memory_space=pl.ANY), pl.BlockSpec(memory_space=pltpu.VMEM)
     widths = [width for _, width, _ in PARTS]
     back = [pltpu.VMEM((8, RING, RING, SLOTS, width), jnp.bfloat16) for width in widths]
@@ -357,37 +461,15 @@
     dma = pltpu.SemaphoreType.DMA
     return pl.pallas_call(
         return_kernel,
-        out_shape=(y, y),
-        in_specs=[vmem_spec] + [any_spec] * 2 + [vmem_spec] * 4,
-        out_specs=(vmem_spec, vmem_spec),
-        scratch_shapes=back * 2 + rows * 2 + sums * 2 + sums * 2
-        + [dma((2, 3, RING)), dma((2, 3)), dma((2, 3)), dma((2, 3, 3)), dma((2, 3)), dma((2, 3, 3)), dma((2, 3))],
-        compiler_params=pltpu.CompilerParams(collective_id=1, has_side_effects=True, vmem_limit_bytes=60 * 1024 * 1024),
+        out_shape=(y, y, jax.ShapeDtypeStruct(x_b.shape, x_b.dtype)),
+        in_specs=[vmem_spec] + [any_spec] * 2 + [vmem_spec] * 4 + [any_spec] * 3,
+        out_specs=(vmem_spec, vmem_spec, any_spec),
+        scratch_shapes=back * 2 + rows * 2 + sums * 3 + [pltpu.VMEM((tokens, model), jnp.float32)]
+        + [dma((2, 3, RING)), dma((2, 3)), dma((2, 3)), dma((2, 3, 3)), dma((2, 3)), dma((2, 3, 3)), dma((3,))]
+        + expert_scratch(model, ffn),
+        compiler_params=pltpu.CompilerParams(collective_id=1, has_side_effects=True, vmem_limit_bytes=63 * 1024 * 1024),
         name="return_rows",
-    )(ids, *outs, *metas, *residuals)
-
-
-def ffn_kernel(x_ref, wg_ref, wu_ref, wd_ref, o_ref):
-    x = x_ref[...].reshape(-1, wg_ref.shape[0])
-    gate_act = jnp.dot(x, wg_ref[...], preferred_element_type=jnp.float32)
-    up_act = jnp.dot(x, wu_ref[...], preferred_element_type=jnp.float32)
-    hidden = (jax.nn.silu(gate_act) * up_act).astype(jnp.bfloat16)
-    o_ref[...] = jnp.dot(hidden, wd_ref[...], preferred_element_type=jnp.float32).astype(jnp.bfloat16).reshape(o_ref.shape)
-
-
-def expert_ffn(x, w_gate, w_up, w_down):
-    model, ffn = w_gate.shape
-    block = pl.BlockSpec((1,) + x.shape[1:], lambda i: (i, 0, 0, 0, 0))
-    return pl.pallas_call(
-        ffn_kernel,
-        grid=(RING * CORES,),
-        out_shape=jax.ShapeDtypeStruct(x.shape, x.dtype),
-        in_specs=[block, pl.BlockSpec((model, ffn), lambda i: (0, 0)), pl.BlockSpec((model, ffn), lambda i: (0, 0)), pl.BlockSpec((ffn, model), lambda i: (0, 0))],
-        out_specs=block,
-        compiler_params=pltpu.CompilerParams(vmem_limit_bytes=40 * 1024 * 1024),
-        cost_estimate=pl.CostEstimate(flops=6 * 2048 * model * ffn, bytes_accessed=26 * 1024 * 1024, transcendentals=2048 * ffn),
-        name="expert_ffn",
-    )(x, w_gate, w_up, w_down)
+    )(ids, done_a, x_b, *metas, *residuals, *weights)[:2]
 
 
 def solution(mesh):
@@ -404,10 +486,8 @@
         res_a, res_b, own_a, own_b = attention(
             tokens_a, (experts_a, slots_a, gates_a), tokens_b, (experts_b, slots_b, gates_b), attn_gain, moe_gain, w_query, w_key, w_value, w_out
         )
-        x_a, x_b, meta_a, meta_b = dispatch(own_a, own_b, ids[:, :128])
-        o_a = expert_ffn(x_a, w_gate, w_up, w_down)
-        o_b = expert_ffn(x_b, w_gate, w_up, w_down)
-        y_a, y_b = bring_back(ids, (o_a, o_b), (meta_a, meta_b), (res_a, res_b))
-        return y_a.astype(jnp.bfloat16), y_b.astype(jnp.bfloat16)
+        weights = (w_gate, w_up, w_down)
+        _, x_b, meta_a, meta_b, done_a = dispatch(own_a, own_b, ids[:, :128], weights)
+        return bring_back(ids, done_a, x_b, (meta_a, meta_b), (res_a, res_b), weights)
 
     return jax.shard_map(device_fn, mesh=mesh, in_specs=in_specs, out_specs=(row_spec, row_spec), check_vma=False)

time: 421 us -> 348 us (0.83)
  Pallas kernels: 398 us -> 339 us
  local copies, waits for them, and re-layouts: 17.3 us -> 4.9 us
    pallas_call x4 -> x2, Pallas kernels: 368 us -> 307 us  [the longest x1 170 us: bring_back(): pl.pallas_call(return_kernel, out_shape=(y, y, jax.ShapeDtypeStruct(x_b.s...]
    unnamed x34 -> x4, local copies, waits for them, and re-layouts: 14.7 us -> 3.77 us
where the time goes in v1:
time: 348 us; the launch traced here: 345 us
  Pallas kernels  339 us (97%)
  local copies, waits for them, and re-layouts  4.9 us (1%)
    pallas_call x1, Pallas kernels, bring_back(): pl.pallas_call(return_kernel, out_shape=(y, y, jax.ShapeDtypeStruct(x_b.s...  170 us
    pallas_call x1, Pallas kernels, dispatch(): pl.pallas_call(dispatch_kernel, out_shape=(out, out, meta, meta, out), in...  137 us
    pallas_call x1, Pallas kernels, attention(): pl.pallas_call(attention_kernel, grid=(steps,), out_shape=tuple((jax.Shap...  32.3 us

profile of v1, /device:TPU:0, one launch (start us, length us, event | category | flops | bytes accessed | tf_op | source)
XLA Modules:
  0.0 345.1 jit_solution(15869959016796617060)
XLA Ops:
  0.8 0.1 stack_broadcast_in_dim.6
  0.9 0.1 stack_broadcast_in_dim.8
  1.0 0.1 stack_broadcast_in_dim.7
  1.2 0.1 pad_maximum_fusion.ids_ref
  1.2 0.0 copy-start
  1.2 0.8 slice.4.ids_ref
  2.0 32.3 %attention.1 = (bf16[128,2048]{1,0:T(8,128)(2,1)}, bf16[128,2048]{1,0:T(8,128)(2,1)}, bf16[136,2048]{1,0:T(8,128)(2,1)}, bf16[136,2048]{1,0:T(8,128)(2,1)}) custom-call(bf16[128,2048]{1,0:T(8,128)(2,1)} %xa_ref.1, bf16[128,2048]{1,0:T(8,128)(2,1)} %xb_ref.1, s32[8,128]{1,0:T(8,128)} %bitcast.29, s32[8,128]{1,0:T(8,128)} %bitcast.30, ...), custom_call_target="tpu_custom_call" | custom-call | tf_op jit(solution)/shard_map/attention/pallas_call | solution.py:78
  34.2 0.0 copy-done
  34.2 136.9 %dispatch_rows.1 = (bf16[8,4,4,16,2048]{4,3,2,1,0:T(8,128)(2,1)}, bf16[8,4,4,16,2048]{4,3,2,1,0:T(8,128)(2,1)}, bf16[3,4,8,384]{3,2,1,0:T(8,128)(2,1)}, bf16[3,4...) custom-call(f32[3,128,128]{2,1,0:T(8,128)} %slice.4.ids_ref, bf16[136,2048]{1,0:T(8,128)(2,1)} %get-tuple-element.12.refs_0_, ...), custom_call_target="tpu_custom_call" | custom-call | tf_op jit(solution)/shard_map/dispatch_rows/pallas_call | solution.py:339
  171.2 170.2 %return_rows.1 = (bf16[128,2048]{1,0:T(8,128)(2,1)}, bf16[128,2048]{1,0:T(8,128)(2,1)}, bf16[8,4,4,16,2048]{4,3,2,1,0:T(8,128)(2,1)}) custom-call(f32[3,512,128]{2,1,0:T(8,128)} %copy-done, bf16[8,4,4,16,2048]{4,3,2,1,0:T(8,128)(2,1)} %get-tuple-element.14.refs_0_, bf16[8,4,4,16,2048]{4,3,2,1,0:T(8,128)(2,1)} %get-tuple-element.15.refs_1_, ...), custom_call_target="tpu_custom_call" | custom-call | tf_op jit(solution)/shard_map/return_rows/pallas_call | solution.py:462
  341.3 1.9 copy.21
  343.2 1.9 copy.22
  (2 shorter events, 0.1 us)
Async XLA Ops:
  1.2 33.0 %copy-start = (f32[3,512,128]{2,1,0:T(8,128)}, f32[3,512,128]{2,1,0:T(8,128)S(1)}, u32[]{:S(2)}) copy-start(f32[3,512,128]{2,1,0:T(8,128)S(1)} %pad_maximum_fusion.ids_ref) | copy-start | bytes 2359300

commit v2 on v1

v2 whole, which is shorter than its diff:
```python
import jax
import jax.numpy as jnp
from jax import lax
from jax.experimental import pallas as pl
from jax.experimental.pallas import tpu as pltpu
from jax.sharding import PartitionSpec as P

NORM_EPS = 1e-6
MASK_VALUE = -1e30
RING = 4
CORES = 2
SLOTS = 16
HEAD_DIM = 64
PARTS = (
    (0, 640, ("z", "y", "x")),
    (640, 640, ("x", "z", "y")),
    (1280, 768, ("y", "x", "z")),
)
STRIDE = {"z": 32, "y": 8, "x": 2}

def coords(index):
    return {"z": index // 32, "y": (index // 8) % RING, "x": (index // 2) % RING}, index % CORES


def peer(dim, delta, flip=0):
    me = lax.axis_index("ep")
    stride = STRIDE[dim]
    place = lax.rem(me // stride, RING)
    other = me + (lax.rem(place + delta % RING, RING) - place) * stride
    if flip:
        other = other + 1 - 2 * lax.rem(me, CORES)
    return {"ep": other}


def send(src, dst, send_sem, recv_sem, where):
    return pltpu.make_async_remote_copy(src_ref=src, dst_ref=dst, send_sem=send_sem, recv_sem=recv_sem, device_id=where, device_id_type=pl.DeviceIdType.MESH)


def drain(ref, sem):
    pltpu.make_async_copy(ref, ref, sem).wait()


def greet():
    barrier = pltpu.get_barrier_semaphore()
    count = 0
    for dim in ("x", "y", "z"):
        for delta in range(1, RING):
            for flip in range(CORES):
                pl.semaphore_signal(barrier, inc=1, device_id=peer(dim, delta, flip), device_id_type=pl.DeviceIdType.MESH)
                count += 1
    pl.semaphore_signal(barrier, inc=1, device_id=peer("x", 0, 1), device_id_type=pl.DeviceIdType.MESH)
    return barrier, count + 1


def group_view(rows, part, off3, flip, off2):
    start, width, (_, s2, s3) = PARTS[part]
    place = {s3: off3, s2: off2}
    index = tuple(place.get(dim, slice(None)) for dim in ("y", "z"))
    line = flip * RING + place["x"] if "x" in place else slice(flip * RING, (flip + 1) * RING)
    return rows.at[line, index[0], index[1], :, start : start + width]


def row_ids(order, off2):
    s1, s2, s3 = order
    pos, core = coords(lax.axis_index("ep"))
    row = lax.broadcasted_iota(jnp.int32, (128, 128), 0)
    slot, flip, off3 = row % SLOTS, (row // SLOTS) % CORES, row // (SLOTS * CORES)
    base = pos[s1] * STRIDE[s1] + lax.rem(pos[s2] + off2, RING) * STRIDE[s2] + core
    expert = base + (pos[s3] + off3) % RING * STRIDE[s3] + flip * (1 - 2 * core)
    return (expert * SLOTS + slot).astype(jnp.float32)


PAIRS = tuple((off, flip) for off in range(RING) for flip in range(CORES))


def routing_ids(meta):
    expert = meta[:, 0:128].astype(jnp.float32)
    slot = meta[:, 128:256].astype(jnp.float32)
    return jnp.where(slot >= 0, expert * SLOTS + slot, -1.0)


def rms_norm(rows_f, gain_ref):
    inv_rms = lax.rsqrt(jnp.mean(rows_f * rows_f, axis=-1, keepdims=True) + NORM_EPS)
    return rows_f * inv_rms * gain_ref[...].astype(jnp.float32).reshape(1, -1)


def attend(x_ref, gain_ref, w_refs, pool, sem, normed_t, total, last, between):
    tokens, model = x_ref.shape
    steps = w_refs[0].shape[0]

    def load(i, slot):
        for w, w_ref in enumerate(w_refs):
            pltpu.make_async_copy(w_ref.at[i], pool.at[slot * 4 + w], sem.at[slot]).start()

    normed_t[...] = rms_norm(x_ref[...].astype(jnp.float32), gain_ref).T.astype(jnp.bfloat16)
    total[...] = jnp.zeros_like(total)
    seen = lax.broadcasted_iota(jnp.int32, (tokens, tokens), 0) <= lax.broadcasted_iota(jnp.int32, (tokens, tokens), 1)

    def step(i, carry):
        slot = lax.rem(i, 2)
        if last:

            @pl.when(i + 1 < steps)
            def _():
                load(i + 1, 1 - slot)

        else:
            load(lax.rem(i + 1, steps), 1 - slot)
        drain(pool.at[pl.ds(slot * 4, 4)], sem.at[slot])
        query, keys, values = (
            jnp.dot(pool[slot * 4 + w].reshape(-1, model), normed_t[...], preferred_element_type=jnp.float32).astype(jnp.bfloat16) for w in range(3)
        )
        context = []
        for start in range(0, query.shape[0], HEAD_DIM):
            head = slice(start, start + HEAD_DIM)
            scores = lax.dot_general(keys[head], query[head], (((0,), (0,)), ((), ())), preferred_element_type=jnp.float32) * (HEAD_DIM**-0.5)
            scores = jnp.where(seen, scores, MASK_VALUE)
            weight = jnp.exp(scores - jnp.max(scores, axis=0, keepdims=True))
            prob = (weight / jnp.sum(weight, axis=0, keepdims=True)).astype(jnp.bfloat16)
            context.append(jnp.dot(values[head], prob, preferred_element_type=jnp.float32).astype(jnp.bfloat16))
        context = jnp.concatenate(context, axis=0)
        total[...] += lax.dot_general(context, pool[slot * 4 + 3].reshape(-1, model), (((0,), (0,)), ((), ())), preferred_element_type=jnp.float32)
        between(i)
        return carry

    if not last:
        load(0, 0)
    lax.fori_loop(0, steps, step, 0)


def load_weights(w_refs, held, sem):
    copies = [pltpu.make_async_copy(src, dst, sem.at[i]) for i, (src, dst) in enumerate(zip(w_refs, held))]
    for copy in copies:
        copy.start()
    return copies


def run_experts(x_ref, o_ref, held, pool, x_sem, o_sem, between):
    blocks = x_ref.shape[0]
    gate_w, up_w, down_w = held
    x_buf, o_buf = pool.at[0:2], pool.at[2:4]

    def load(b, slot):
        return pltpu.make_async_copy(x_ref.at[b], x_buf.at[slot], x_sem.at[slot])

    load(0, 0).start()

    def step(b, carry):
        slot = lax.rem(b, 2)

        @pl.when(b + 1 < blocks)
        def _():
            load(b + 1, 1 - slot).start()

        load(b, slot).wait()

        @pl.when(b >= 2)
        def _():
            drain(o_buf.at[slot], o_sem.at[slot])

        x = x_buf[slot].reshape(-1, gate_w.shape[0])
        gate_act = jnp.dot(x, gate_w[...], preferred_element_type=jnp.float32)
        up_act = jnp.dot(x, up_w[...], preferred_element_type=jnp.float32)
        hidden = (jax.nn.silu(gate_act) * up_act).astype(jnp.bfloat16)
        o_buf[slot] = jnp.dot(hidden, down_w[...], preferred_element_type=jnp.float32).astype(jnp.bfloat16).reshape(o_buf.shape[1:])
        pltpu.make_async_copy(o_buf.at[slot], o_ref.at[b], o_sem.at[slot]).start()
        between(b)
        return carry

    lax.fori_loop(0, blocks, step, 0)
    for slot in range(2):
        drain(o_buf.at[slot], o_sem.at[slot])


def expert_scratch(model, ffn):
    dma = pltpu.SemaphoreType.DMA
    return [
        pltpu.VMEM((model, ffn), jnp.bfloat16),
        pltpu.VMEM((model, ffn), jnp.bfloat16),
        pltpu.VMEM((ffn, model), jnp.bfloat16),
        dma((3,)),
        dma((2,)),
        dma((2,)),
    ]


def dispatch_kernel(*refs):
    batches = 2
    x_refs, routing_refs, gain_refs, aw_refs, w_refs = refs[0:2], (refs[2:5], refs[5:8]), refs[8:10], refs[10:14], refs[14:17]
    out_refs, meta_refs, res_refs, done_ref = refs[17:19], refs[19:21], refs[21:23], refs[23]
    scratch = refs[24:]
    planes = [scratch[3 * n : 3 + 3 * n] for n in range(batches)]
    chosen = [scratch[6 + 3 * n : 9 + 3 * n] for n in range(batches)]
    plane_recv, plane_send, row_recv, row_send, local_sem = scratch[12:17]
    own_refs, normed_t, total, ids_ref, pool, attn_sem = scratch[17:19], scratch[19], scratch[20], scratch[21], scratch[22], scratch[23]
    held, (w_sem, x_sem, o_sem) = scratch[24:27], scratch[27:]
    tokens = x_refs[0].shape[0]
    half = tokens // 2
    barrier, greetings = greet()

    def own_part(n, part):
        start, width, _ = PARTS[part]
        return own_refs[n].at[:, start : start + width]

    def attention(n, between):
        attend(x_refs[n], gain_refs[0], aw_refs, pool, attn_sem, normed_t, total, n == batches - 1, between)
        residual = (x_refs[n][...].astype(jnp.float32) + total[...]).astype(jnp.bfloat16)
        res_refs[n][...] = residual
        own_refs[n][0:tokens, :] = rms_norm(residual.astype(jnp.float32), gain_refs[1]).astype(jnp.bfloat16)
        own_refs[n][tokens : tokens + 8, :] = jnp.zeros((8, own_refs[n].shape[1]), jnp.bfloat16)
        for start, _, _ in PARTS:
            for i, ref in enumerate(routing_refs[n]):
                own_refs[n][tokens : tokens + 8, start + i * 128 : start + (i + 1) * 128] = ref[...].astype(jnp.float32).astype(jnp.bfloat16)

    def send_own(n):
        for part, (_, _, (s1, s2, _)) in enumerate(PARTS):
            plane = planes[n][part]
            for off in (1, 3, 2):
                send(own_part(n, part), plane.at[off], plane_send.at[n, part], plane_recv.at[n, part, off], peer(s1, off)).start()
            for off in (1, 3):
                send(own_part(n, part), plane.at[off * RING], plane_send.at[n, part], plane_recv.at[n, part, off * RING], peer(s2, off)).start()

    def forward(n):
        for part, (_, _, (s1, s2, _)) in enumerate(PARTS):
            plane = planes[n][part]
            for off1 in (1, 3, 2):
                drain(plane.at[off1], plane_recv.at[n, part, off1])
                for off2 in (1, 3):
                    send(plane.at[off1], plane.at[off2 * RING + off1], plane_send.at[n, part], plane_recv.at[n, part, off2 * RING + off1], peer(s2, off2)).start()

    def relay(n, off2):
        rows = slice(0, half) if off2 == 1 else slice(half, tokens + 8)
        for part, (_, _, (s1, s2, _)) in enumerate(PARTS):
            plane = planes[n][part]
            for off1 in range(RING):
                drain(plane.at[off2 * RING + off1], plane_recv.at[n, part, off2 * RING + off1])
                send(plane.at[off2 * RING + off1, rows], plane.at[2 * RING + off1, rows], plane_send.at[n, part], plane_recv.at[n, part, 2 * RING + off1], peer(s2, off2)).start()

    def select(n, part, off2, off1, block):
        width = PARTS[part][1]
        ids = ids_ref[part]
        dest = routing_ids(block[tokens : tokens + 8, 0:384])
        hit = ids == dest[0:1, :]
        for j in range(1, 8):
            hit = jnp.logical_or(hit, ids == dest[j : j + 1, :])
        onehot = jnp.where(hit, 1.0, 0.0).astype(jnp.bfloat16)
        rows = jnp.dot(onehot, block[0:tokens, :], preferred_element_type=jnp.float32).astype(jnp.bfloat16)
        chosen[n][part][:, off2, off1] = rows.reshape(8, SLOTS, width)

    def select_group(n, part, off2):
        start, width, _ = PARTS[part]
        plane = planes[n][part]
        if off2 == 0:
            meta_refs[n][part, 0] = own_refs[n][tokens : tokens + 8, start : start + 384]
            for off1 in range(1, RING):
                meta_refs[n][part, off1] = plane[off1, tokens : tokens + 8, 0:384]
            select(n, part, 0, 0, own_refs[n].at[:, start : start + width])
            first = 1
        else:
            for off1 in range(RING if off2 == 2 else 0):
                drain(plane.at[off2 * RING + off1], plane_recv.at[n, part, off2 * RING + off1])
            first = 0

        def body(off1, carry):
            select(n, part, off2, off1, plane.at[off2 * RING + off1])
            return carry

        lax.fori_loop(first, RING, body, 0)

    def send_group(n, part, off2):
        s3 = PARTS[part][2][2]
        for i in (2, 3, 6, 7, 4, 5, 1):
            off3, flip = PAIRS[i]
            send(chosen[n][part].at[i, off2], group_view(out_refs[n], part, off3, flip, off2), row_send.at[n, part], row_recv.at[n], peer(s3, off3, flip)).start()
        pltpu.make_async_copy(chosen[n][part].at[0, off2], group_view(out_refs[n], part, 0, 0, off2), local_sem.at[n, part]).start()

    late = []

    def groups(n, off2):
        for part in range(3):
            select_group(n, part, off2)
            if late:
                send_group(*late.pop())
            late.append((n, part, off2))

    def flush():
        if late:
            send_group(*late.pop())

    def under_b(i):
        @pl.when(i == 4)
        def _():
            forward(0)

        @pl.when(i == 5)
        def _():
            groups(0, 0)

        @pl.when(i == 6)
        def _():
            flush()

    attention(0, lambda i: None)
    for part, (_, _, order) in enumerate(PARTS):
        ids_ref[part] = row_ids(order, 0)
    pl.semaphore_wait(barrier, greetings)
    send_own(0)
    attention(1, under_b)
    weight_copies = load_weights(w_refs, held, w_sem)
    send_own(1)
    relay(0, 1)
    relay(0, 3)
    groups(0, 1)
    groups(0, 3)
    forward(1)
    flush()
    groups(0, 2)
    groups(1, 0)
    relay(1, 1)
    relay(1, 3)
    flush()
    for off2 in (1, 3, 2):
        groups(1, off2)
    flush()

    def rows_done(n):
        drain(out_refs[n].at[1:8], row_recv.at[n])
        for part in range(3):
            drain(chosen[n][part].at[0], local_sem.at[n, part])

    rows_done(0)
    for copy in weight_copies:
        copy.wait()
    run_experts(out_refs[0], done_ref, held, pool, x_sem, o_sem, lambda b: None)
    rows_done(1)
    for n in range(batches):
        for part in range(3):
            drain(planes[n][part].at[1:16], plane_send.at[n, part])
            drain(chosen[n][part].at[1:8], row_send.at[n, part])


def dispatch(tokens, routing, gains, attention_weights, weights):
    rows, model = tokens[0].shape
    ffn = weights[0].shape[1]
    block = (RING, RING, SLOTS, model)
    out = jax.ShapeDtypeStruct((CORES * RING,) + block, jnp.bfloat16)
    meta = jax.ShapeDtypeStruct((3, RING, 8, 384), jnp.bfloat16)
    residual = jax.ShapeDtypeStruct((rows, model), jnp.bfloat16)
    any_spec, vmem_spec = pl.BlockSpec(memory_space=pl.ANY), pl.BlockSpec(memory_space=pltpu.VMEM)
    plane = [pltpu.VMEM((RING * RING, rows + 8, width), jnp.bfloat16) for _, width, _ in PARTS]
    chosen = [pltpu.VMEM((8, RING, RING, SLOTS, width), jnp.bfloat16) for _, width, _ in PARTS]
    own = pltpu.VMEM((rows + 8, model), jnp.bfloat16)
    dma = pltpu.SemaphoreType.DMA
    return pl.pallas_call(
        dispatch_kernel,
        out_shape=(out, out, meta, meta, residual, residual, out),
        in_specs=[vmem_spec] * 10 + [any_spec] * 7,
        out_specs=(any_spec,) * 2 + (vmem_spec,) * 4 + (any_spec,),
        scratch_shapes=plane * 2
        + chosen * 2
        + [dma((2, 3, 16)), dma((2, 3)), dma((2,)), dma((2, 3)), dma((2, 3))]
        + [own, own, pltpu.VMEM((model, rows), jnp.bfloat16), pltpu.VMEM((rows, model), jnp.float32), pltpu.VMEM((3, 128, 128), jnp.float32)]
        + [pltpu.VMEM((8,) + block, jnp.bfloat16), dma((2,))]
        + expert_scratch(model, ffn),
        compiler_params=pltpu.CompilerParams(collective_id=0, has_side_effects=True, vmem_limit_bytes=63 * 1024 * 1024),
        name="dispatch_rows",
    )(*tokens, *routing[0], *routing[1], *gains, *(w.reshape((8,) + block) for w in attention_weights), *weights)


def return_kernel(*refs):
    batches = 2
    done_a, x_b, meta_refs, res_refs, w_refs = refs[0], refs[1], refs[2:4], refs[4:6], refs[6:9]
    y_refs, done_b, scratch = refs[9:11], refs[11], refs[12:]
    out_refs = (done_a, done_b)
    back = [scratch[0 + 3 * n : 3 + 3 * n] for n in range(batches)]
    rows = [scratch[6 + 3 * n : 9 + 3 * n] for n in range(batches)]
    sums, got = scratch[12:15], [scratch[15 + 3 * n : 18 + 3 * n] for n in range(batches)]
    kept = scratch[21]
    back_recv, back_send, own_sem, rows_recv, rows_send, sums_recv, sums_send = scratch[22:29]
    ids_ref, pool = scratch[29:31]
    held, (w_sem, x_sem, o_sem) = scratch[31:34], scratch[34:]
    tokens = y_refs[0].shape[0]
    barrier, greetings = greet()
    for part, (_, _, order) in enumerate(PARTS):
        for off2 in range(RING):
            ids_ref[part, off2] = row_ids(order, off2)
    pl.semaphore_wait(barrier, greetings)
    weight_copies = load_weights(w_refs, held, w_sem)

    def hand_out(n):
        for part in range(3):
            for off2 in range(RING):
                pltpu.make_async_copy(group_view(out_refs[n], part, 0, 0, off2), back[n][part].at[0, off2], own_sem.at[n, part]).start()
        for off2 in (2, 1, 3, 0):
            for i in (2, 3, 6, 7, 4, 5, 1):
                off3, flip = PAIRS[i]
                for part in range(3):
                    s3 = PARTS[part][2][2]
                    send(group_view(out_refs[n], part, off3, flip, off2), back[n][part].at[i, off2], back_send.at[n, part], back_recv.at[n, part, off2], peer(s3, -off3, flip)).start()

    def turn(n, off2):
        for part in range(3):
            s2 = PARTS[part][2][1]
            drain(back[n][part].at[1:8, off2], back_recv.at[n, part, off2])
            if off2:
                send(back[n][part].at[:, off2], rows[n][part].at[off2 - 1], rows_send.at[n, part], rows_recv.at[n, part, off2 - 1], peer(s2, -off2)).start()

    def weighted(n, part, off2, off1):
        width = PARTS[part][1]
        meta = meta_refs[n][part, off1]
        dest = routing_ids(meta)
        gates = meta[:, 256:384].astype(jnp.float32)
        ids = ids_ref[part, off2]
        weight = jnp.zeros((128, tokens), jnp.float32)
        for j in range(8):
            weight = jnp.where(ids == dest[j : j + 1, :], gates[j : j + 1, :], weight)
        block = back[n][part][:, 0, off1] if off2 == 0 else rows[n][part][off2 - 1, :, off1]
        return lax.dot_general(weight.astype(jnp.bfloat16), block.reshape(128, width), (((0,), (0,)), ((), ())), preferred_element_type=jnp.float32)

    def own_ready(n):
        for part in range(3):
            drain(back[n][part].at[0], own_sem.at[n, part])

    def add_group(n, off2, first=False, last=False):
        late = []

        def flush():
            if late:
                part, off1 = late.pop()
                s1 = PARTS[part][2][0]
                send(sums[part].at[off1 - 1], got[n][part].at[off1 - 1], sums_send.at[part], sums_recv.at[n, part, off1 - 1], peer(s1, -off1)).start()

        for part in range(3):
            start, width, _ = PARTS[part]
            if off2:
                drain(rows[n][part].at[off2 - 1], rows_recv.at[n, part, off2 - 1])
            for off1 in (2, 1, 3, 0):
                term = weighted(n, part, off2, off1)
                if off1 == 0:
                    before = res_refs[n][:, start : start + width].astype(jnp.float32) if first else kept[:, start : start + width]
                    kept[:, start : start + width] = before + term
                else:
                    sums[part][off1 - 1] = term if first else sums[part][off1 - 1] + term
                flush()
                if last and off1:
                    late.append((part, off1))

    def finish(n):
        for part in range(3):
            start, width, _ = PARTS[part]
            total = kept[:, start : start + width]
            for off1 in range(1, RING):
                drain(got[n][part].at[off1 - 1], sums_recv.at[n, part, off1 - 1])
                total = total + got[n][part][off1 - 1]
            y_refs[n][:, start : start + width] = total.astype(y_refs[n].dtype)
            drain(sums[part], sums_send.at[part])

    hand_out(0)
    for copy in weight_copies:
        copy.wait()

    def between(b):
        for when, off2 in ((1, 2), (3, 1), (5, 3), (7, 0)):

            @pl.when(b == when)
            def _():
                if off2 == 2:
                    own_ready(0)
                turn(0, off2)

    run_experts(x_b, done_b, held, pool, x_sem, o_sem, between)
    hand_out(1)
    add_group(0, 0, first=True)
    add_group(0, 2)
    add_group(0, 1)
    own_ready(1)
    turn(1, 2)
    add_group(0, 3, last=True)
    for off2 in (1, 3, 0):
        turn(1, off2)
    finish(0)
    add_group(1, 0, first=True)
    add_group(1, 2)
    add_group(1, 1)
    add_group(1, 3, last=True)
    finish(1)
    for n in range(batches):
        for part in range(3):
            drain(back[n][part].at[1:8], back_send.at[n, part])
            drain(rows[n][part], rows_send.at[n, part])


def bring_back(done_a, x_b, metas, residuals, weights):
    tokens, model = residuals[0].shape
    ffn = weights[0].shape[1]
    y = jax.ShapeDtypeStruct((tokens, model), jnp.bfloat16)
    any_spec, vmem_spec = pl.BlockSpec(memory_space=pl.ANY), pl.BlockSpec(memory_space=pltpu.VMEM)
    widths = [width for _, width, _ in PARTS]
    back = [pltpu.VMEM((8, RING, RING, SLOTS, width), jnp.bfloat16) for width in widths]
    rows = [pltpu.VMEM((RING - 1, 8, RING, SLOTS, width), jnp.bfloat16) for width in widths]
    sums = [pltpu.VMEM((RING - 1, tokens, width), jnp.float32) for width in widths]
    dma = pltpu.SemaphoreType.DMA
    return pl.pallas_call(
        return_kernel,
        out_shape=(y, y, jax.ShapeDtypeStruct(x_b.shape, x_b.dtype)),
        in_specs=[any_spec] * 2 + [vmem_spec] * 4 + [any_spec] * 3,
        out_specs=(vmem_spec, vmem_spec, any_spec),
        scratch_shapes=back * 2 + rows * 2 + sums * 3 + [pltpu.VMEM((tokens, model), jnp.float32)]
        + [dma((2, 3, RING)), dma((2, 3)), dma((2, 3)), dma((2, 3, 3)), dma((2, 3)), dma((2, 3, 3)), dma((3,))]
        + [pltpu.VMEM((3, RING, 128, 128), jnp.float32), pltpu.VMEM((4,) + x_b.shape[1:], jnp.bfloat16)]
        + expert_scratch(model, ffn),
        compiler_params=pltpu.CompilerParams(collective_id=1, has_side_effects=True, vmem_limit_bytes=63 * 1024 * 1024),
        name="return_rows",
    )(done_a, x_b, *metas, *residuals, *weights)[:2]


def solution(mesh):
    row_spec = P(("dp", "ep"), None)
    full_spec = P(None, None, None)
    gain_spec = P(None)
    expert_spec = P("ep", None, None)
    in_specs = (row_spec,) * 8 + (gain_spec,) + (full_spec,) * 4 + (gain_spec,) + (expert_spec,) * 3

    def device_fn(tokens_a, experts_a, slots_a, gates_a, tokens_b, experts_b, slots_b, gates_b, attn_gain, w_query, w_key, w_value, w_out, moe_gain, w_gate, w_up, w_down):
        weights = (w_gate[0], w_up[0], w_down[0])
        attention_weights = [jnp.transpose(w, (1, 2, 0)) for w in (w_query, w_key, w_value)] + [w_out]
        routing = [(e.T, s.T, g.T) for e, s, g in ((experts_a, slots_a, gates_a), (experts_b, slots_b, gates_b))]
        _, x_b, meta_a, meta_b, res_a, res_b, done_a = dispatch((tokens_a, tokens_b), routing, (attn_gain, moe_gain), attention_weights, weights)
        return bring_back(done_a, x_b, (meta_a, meta_b), (res_a, res_b), weights)

    return jax.shard_map(device_fn, mesh=mesh, in_specs=in_specs, out_specs=(row_spec, row_spec), check_vma=False)
```

time: 348 us -> 330 us (0.948)
  Pallas kernels: 339 us -> 326 us
    pallas_call x2 -> x1, Pallas kernels: 169 us -> 157 us  [dispatch(): pl.pallas_call(dispatch_kernel, out_shape=(out, out, meta, meta, residual...]
where the time goes in v2:
time: 330 us
  Pallas kernels  326 us (99%)
  local copies, waits for them, and re-layouts  3.76 us (1%)
    pallas_call x1, Pallas kernels, bring_back(): pl.pallas_call(return_kernel, out_shape=(y, y, jax.ShapeDtypeStruct(x_b.s...  169 us
    pallas_call x1, Pallas kernels, dispatch(): pl.pallas_call(dispatch_kernel, out_shape=(out, out, meta, meta, residual...  157 us

profile of v2, /device:TPU:0, one launch (start us, length us, event | category | flops | bytes accessed | tf_op | source)
XLA Modules:
  0.0 330.0 jit_solution(15525114213761014605)
XLA Ops:
  0.6 156.5 %dispatch_rows.1 = (bf16[8,4,4,16,2048]{4,3,2,1,0:T(8,128)(2,1)}, bf16[8,4,4,16,2048]{4,3,2,1,0:T(8,128)(2,1)}, bf16[3,4,8,384]{3,2,1,0:T(8,128)(2,1)}, bf16[3,4...) custom-call(bf16[128,2048]{1,0:T(8,128)(2,1)} %refs_0_.1, ...), custom_call_target="tpu_custom_call" | custom-call | tf_op jit(solution)/shard_map/dispatch_rows/pallas_call | solution.py:354
  157.2 169.0 %return_rows.1 = (bf16[128,2048]{1,0:T(8,128)(2,1)}, bf16[128,2048]{1,0:T(8,128)(2,1)}, bf16[8,4,4,16,2048]{4,3,2,1,0:T(8,128)(2,1)}) custom-call(bf16[8,4,4,16,2048]{4,3,2,1,0:T(8,128)(2,1)} %get-tuple-element.10.refs_0_, bf16[8,4,4,16,2048]{4,3,2,1,0:T(8,128)(2,1)} %get-tuple-element.11.refs_1_, bf16[3,4,8,384]{3,2,1,0:T(8,128)(2,1)} %get-tuple-element.12.refs_2_, ...), custom_call_target="tpu_custom_call" | custom-call | tf_op jit(solution)/shard_map/return_rows/pallas_call | solution.py:503
  326.2 1.9 copy.21
  328.1 1.9 copy.22

commit v3 on v2

--- a/solution.py
+++ b/solution.py
@@ -215,16 +215,19 @@
     def send_own(n):
         for part, (_, _, (s1, s2, _)) in enumerate(PARTS):
             plane = planes[n][part]
-            for off in (1, 3, 2):
+            for off in (1, 3):
                 send(own_part(n, part), plane.at[off], plane_send.at[n, part], plane_recv.at[n, part, off], peer(s1, off)).start()
             for off in (1, 3):
                 send(own_part(n, part), plane.at[off * RING], plane_send.at[n, part], plane_recv.at[n, part, off * RING], peer(s2, off)).start()
 
-    def forward(n):
+    def forward(n, far):
         for part, (_, _, (s1, s2, _)) in enumerate(PARTS):
             plane = planes[n][part]
-            for off1 in (1, 3, 2):
+            for off1 in (2,) if far else (1, 3):
                 drain(plane.at[off1], plane_recv.at[n, part, off1])
+                if not far:
+                    rows = slice(0, half) if off1 == 1 else slice(half, tokens + 8)
+                    send(plane.at[off1, rows], plane.at[2, rows], plane_send.at[n, part], plane_recv.at[n, part, 2], peer(s1, off1)).start()
                 for off2 in (1, 3):
                     send(plane.at[off1], plane.at[off2 * RING + off1], plane_send.at[n, part], plane_recv.at[n, part, off2 * RING + off1], peer(s2, off2)).start()
 
@@ -288,17 +291,13 @@
             send_group(*late.pop())
 
     def under_b(i):
-        @pl.when(i == 4)
-        def _():
-            forward(0)
-
-        @pl.when(i == 5)
-        def _():
-            groups(0, 0)
+        @pl.when(i == 2)
+        def _():
+            forward(0, False)
 
         @pl.when(i == 6)
         def _():
-            flush()
+            forward(0, True)
 
     attention(0, lambda i: None)
     for part, (_, _, order) in enumerate(PARTS):
@@ -308,30 +307,44 @@
     attention(1, under_b)
     weight_copies = load_weights(w_refs, held, w_sem)
     send_own(1)
+    groups(0, 0)
     relay(0, 1)
     relay(0, 3)
     groups(0, 1)
+    forward(1, False)
     groups(0, 3)
-    forward(1)
+    forward(1, True)
     flush()
     groups(0, 2)
     groups(1, 0)
     relay(1, 1)
     relay(1, 3)
     flush()
-    for off2 in (1, 3, 2):
-        groups(1, off2)
-    flush()
+    groups(1, 1)
 
     def rows_done(n):
         drain(out_refs[n].at[1:8], row_recv.at[n])
         for part in range(3):
             drain(chosen[n][part].at[0], local_sem.at[n, part])
 
+    def under_a(b):
+        @pl.when(b == 1)
+        def _():
+            groups(1, 3)
+
+        @pl.when(b == 4)
+        def _():
+            groups(1, 2)
+
+        @pl.when(b == 5)
+        def _():
+            flush()
+
+    flush()
     rows_done(0)
     for copy in weight_copies:
         copy.wait()
-    run_experts(out_refs[0], done_ref, held, pool, x_sem, o_sem, lambda b: None)
+    run_experts(out_refs[0], done_ref, held, pool, x_sem, o_sem, under_a)
     rows_done(1)
     for n in range(batches):
         for part in range(3):
@@ -426,9 +439,10 @@
 
         def flush():
             if late:
-                part, off1 = late.pop()
+                part = late.pop()
                 s1 = PARTS[part][2][0]
-                send(sums[part].at[off1 - 1], got[n][part].at[off1 - 1], sums_send.at[part], sums_recv.at[n, part, off1 - 1], peer(s1, -off1)).start()
+                for rows_half, off in ((slice(0, tokens // 2), -1), (slice(tokens // 2, tokens), 1)):
+                    send(sums[part].at[1, rows_half], got[n][part].at[2, rows_half], sums_send.at[part], sums_recv.at[n, part, 2], peer(s1, off)).start()
 
         for part in range(3):
             start, width, _ = PARTS[part]
@@ -442,16 +456,31 @@
                 else:
                     sums[part][off1 - 1] = term if first else sums[part][off1 - 1] + term
                 flush()
-                if last and off1:
-                    late.append((part, off1))
+                if last and off1 == 2:
+                    late.append(part)
+
+    def pass_on(n):
+        def out(part):
+            s1 = PARTS[part][2][0]
+            for off1, place in ((1, 0), (3, 1)):
+                send(sums[part].at[off1 - 1], got[n][part].at[place], sums_send.at[part], sums_recv.at[n, part, place], peer(s1, -off1)).start()
+
+        middle = tokens // 2
+        for part in range(3):
+            drain(got[n][part].at[2], sums_recv.at[n, part, 2])
+            sums[part][0, 0:middle] = sums[part][0, 0:middle] + got[n][part][2, 0:middle]
+            sums[part][2, middle:] = sums[part][2, middle:] + got[n][part][2, middle:]
+            if part:
+                out(part - 1)
+        out(2)
 
     def finish(n):
         for part in range(3):
             start, width, _ = PARTS[part]
             total = kept[:, start : start + width]
-            for off1 in range(1, RING):
-                drain(got[n][part].at[off1 - 1], sums_recv.at[n, part, off1 - 1])
-                total = total + got[n][part][off1 - 1]
+            for place in range(2):
+                drain(got[n][part].at[place], sums_recv.at[n, part, place])
+                total = total + got[n][part][place]
             y_refs[n][:, start : start + width] = total.astype(y_refs[n].dtype)
             drain(sums[part], sums_send.at[part])
 
@@ -460,7 +489,7 @@
         copy.wait()
 
     def between(b):
-        for when, off2 in ((1, 2), (3, 1), (5, 3), (7, 0)):
+        for when, off2 in ((2, 2), (4, 1), (6, 3)):
 
             @pl.when(b == when)
             def _():
@@ -470,19 +499,23 @@
 
     run_experts(x_b, done_b, held, pool, x_sem, o_sem, between)
     hand_out(1)
+    turn(0, 0)
     add_group(0, 0, first=True)
     add_group(0, 2)
     add_group(0, 1)
     own_ready(1)
     turn(1, 2)
     add_group(0, 3, last=True)
-    for off2 in (1, 3, 0):
-        turn(1, off2)
+    turn(1, 1)
+    pass_on(0)
+    turn(1, 3)
+    turn(1, 0)
     finish(0)
     add_group(1, 0, first=True)
     add_group(1, 2)
     add_group(1, 1)
     add_group(1, 3, last=True)
+    pass_on(1)
     finish(1)
     for n in range(batches):
         for part in range(3):

time: 330 us -> 324 us (0.982)
  Pallas kernels: 326 us -> 319 us
    pallas_call x1, Pallas kernels: 169 us -> 165 us  [bring_back(): pl.pallas_call(return_kernel, out_shape=(y, y, jax.ShapeDtypeStruct(x_b.s...]
where the time goes in v3:
time: 324 us; the launch traced here: 323 us
  Pallas kernels  319 us (98%)
  local copies, waits for them, and re-layouts  3.76 us (1%)
    pallas_call x1, Pallas kernels, bring_back(): pl.pallas_call(return_kernel, out_shape=(y, y, jax.ShapeDtypeStruct(x_b.s...  165 us
    pallas_call x1, Pallas kernels, dispatch(): pl.pallas_call(dispatch_kernel, out_shape=(out, out, meta, meta, residual...  154 us

profile of v3, /device:TPU:0, one launch (start us, length us, event | category | flops | bytes accessed | tf_op | source)
XLA Modules:
  0.0 323.4 jit_solution(14537175908321346028)
XLA Ops:
  0.6 154.0 %dispatch_rows.1 = (bf16[8,4,4,16,2048]{4,3,2,1,0:T(8,128)(2,1)}, bf16[8,4,4,16,2048]{4,3,2,1,0:T(8,128)(2,1)}, bf16[3,4,8,384]{3,2,1,0:T(8,128)(2,1)}, bf16[3,4...) custom-call(bf16[128,2048]{1,0:T(8,128)(2,1)} %refs_0_.1, ...), custom_call_target="tpu_custom_call" | custom-call | tf_op jit(solution)/shard_map/dispatch_rows/pallas_call | solution.py:367
  154.6 165.0 %return_rows.1 = (bf16[128,2048]{1,0:T(8,128)(2,1)}, bf16[128,2048]{1,0:T(8,128)(2,1)}, bf16[8,4,4,16,2048]{4,3,2,1,0:T(8,128)(2,1)}) custom-call(bf16[8,4,4,16,2048]{4,3,2,1,0:T(8,128)(2,1)} %get-tuple-element.10.refs_0_, bf16[8,4,4,16,2048]{4,3,2,1,0:T(8,128)(2,1)} %get-tuple-element.11.refs_1_, bf16[3,4,8,384]{3,2,1,0:T(8,128)(2,1)} %get-tuple-element.12.refs_2_, ...), custom_call_target="tpu_custom_call" | custom-call | tf_op jit(solution)/shard_map/return_rows/pallas_call | solution.py:536
  319.6 1.9 copy.21
  321.5 1.9 copy.22

commit v4 on v3

--- a/solution.py
+++ b/solution.py
@@ -11,10 +11,10 @@
 CORES = 2
 SLOTS = 16
 HEAD_DIM = 64
+ORDERS = (("z", "y", "x"), ("x", "z", "y"), ("y", "x", "z"))
 PARTS = (
-    (0, 640, ("z", "y", "x")),
-    (640, 640, ("x", "z", "y")),
-    (1280, 768, ("y", "x", "z")),
+    ((0, 640, ORDERS[0]), (640, 640, ORDERS[1]), (1280, 768, ORDERS[2])),
+    ((0, 768, ORDERS[0]), (768, 640, ORDERS[1]), (1408, 640, ORDERS[2])),
 )
 STRIDE = {"z": 32, "y": 8, "x": 2}
 
@@ -52,8 +52,8 @@
     return barrier, count + 1
 
 
-def group_view(rows, part, off3, flip, off2):
-    start, width, (_, s2, s3) = PARTS[part]
+def group_view(rows, n, part, off3, flip, off2):
+    start, width, (_, s2, s3) = PARTS[n][part]
     place = {s3: off3, s2: off2}
     index = tuple(place.get(dim, slice(None)) for dim in ("y", "z"))
     line = flip * RING + place["x"] if "x" in place else slice(flip * RING, (flip + 1) * RING)
@@ -199,7 +199,7 @@
     barrier, greetings = greet()
 
     def own_part(n, part):
-        start, width, _ = PARTS[part]
+        start, width, _ = PARTS[n][part]
         return own_refs[n].at[:, start : start + width]
 
     def attention(n, between):
@@ -208,12 +208,12 @@
         res_refs[n][...] = residual
         own_refs[n][0:tokens, :] = rms_norm(residual.astype(jnp.float32), gain_refs[1]).astype(jnp.bfloat16)
         own_refs[n][tokens : tokens + 8, :] = jnp.zeros((8, own_refs[n].shape[1]), jnp.bfloat16)
-        for start, _, _ in PARTS:
+        for start, _, _ in PARTS[n]:
             for i, ref in enumerate(routing_refs[n]):
                 own_refs[n][tokens : tokens + 8, start + i * 128 : start + (i + 1) * 128] = ref[...].astype(jnp.float32).astype(jnp.bfloat16)
 
     def send_own(n):
-        for part, (_, _, (s1, s2, _)) in enumerate(PARTS):
+        for part, (_, _, (s1, s2, _)) in enumerate(PARTS[n]):
             plane = planes[n][part]
             for off in (1, 3):
                 send(own_part(n, part), plane.at[off], plane_send.at[n, part], plane_recv.at[n, part, off], peer(s1, off)).start()
@@ -221,7 +221,7 @@
                 send(own_part(n, part), plane.at[off * RING], plane_send.at[n, part], plane_recv.at[n, part, off * RING], peer(s2, off)).start()
 
     def forward(n, far):
-        for part, (_, _, (s1, s2, _)) in enumerate(PARTS):
+        for part, (_, _, (s1, s2, _)) in enumerate(PARTS[n]):
             plane = planes[n][part]
             for off1 in (2,) if far else (1, 3):
                 drain(plane.at[off1], plane_recv.at[n, part, off1])
@@ -233,14 +233,14 @@
 
     def relay(n, off2):
         rows = slice(0, half) if off2 == 1 else slice(half, tokens + 8)
-        for part, (_, _, (s1, s2, _)) in enumerate(PARTS):
+        for part, (_, _, (s1, s2, _)) in enumerate(PARTS[n]):
             plane = planes[n][part]
             for off1 in range(RING):
                 drain(plane.at[off2 * RING + off1], plane_recv.at[n, part, off2 * RING + off1])
                 send(plane.at[off2 * RING + off1, rows], plane.at[2 * RING + off1, rows], plane_send.at[n, part], plane_recv.at[n, part, 2 * RING + off1], peer(s2, off2)).start()
 
     def select(n, part, off2, off1, block):
-        width = PARTS[part][1]
+        width = PARTS[n][part][1]
         ids = ids_ref[part]
         dest = routing_ids(block[tokens : tokens + 8, 0:384])
         hit = ids == dest[0:1, :]
@@ -251,7 +251,7 @@
         chosen[n][part][:, off2, off1] = rows.reshape(8, SLOTS, width)
 
     def select_group(n, part, off2):
-        start, width, _ = PARTS[part]
+        start, width, _ = PARTS[n][part]
         plane = planes[n][part]
         if off2 == 0:
             meta_refs[n][part, 0] = own_refs[n][tokens : tokens + 8, start : start + 384]
@@ -271,11 +271,11 @@
         lax.fori_loop(first, RING, body, 0)
 
     def send_group(n, part, off2):
-        s3 = PARTS[part][2][2]
+        s3 = ORDERS[part][2]
         for i in (2, 3, 6, 7, 4, 5, 1):
             off3, flip = PAIRS[i]
-            send(chosen[n][part].at[i, off2], group_view(out_refs[n], part, off3, flip, off2), row_send.at[n, part], row_recv.at[n], peer(s3, off3, flip)).start()
-        pltpu.make_async_copy(chosen[n][part].at[0, off2], group_view(out_refs[n], part, 0, 0, off2), local_sem.at[n, part]).start()
+            send(chosen[n][part].at[i, off2], group_view(out_refs[n], n, part, off3, flip, off2), row_send.at[n, part], row_recv.at[n], peer(s3, off3, flip)).start()
+        pltpu.make_async_copy(chosen[n][part].at[0, off2], group_view(out_refs[n], n, part, 0, 0, off2), local_sem.at[n, part]).start()
 
     late = []
 
@@ -300,7 +300,7 @@
             forward(0, True)
 
     attention(0, lambda i: None)
-    for part, (_, _, order) in enumerate(PARTS):
+    for part, order in enumerate(ORDERS):
         ids_ref[part] = row_ids(order, 0)
     pl.semaphore_wait(barrier, greetings)
     send_own(0)
@@ -360,8 +360,9 @@
     meta = jax.ShapeDtypeStruct((3, RING, 8, 384), jnp.bfloat16)
     residual = jax.ShapeDtypeStruct((rows, model), jnp.bfloat16)
     any_spec, vmem_spec = pl.BlockSpec(memory_space=pl.ANY), pl.BlockSpec(memory_space=pltpu.VMEM)
-    plane = [pltpu.VMEM((RING * RING, rows + 8, width), jnp.bfloat16) for _, width, _ in PARTS]
-    chosen = [pltpu.VMEM((8, RING, RING, SLOTS, width), jnp.bfloat16) for _, width, _ in PARTS]
+    widths = [width for parts in PARTS for _, width, _ in parts]
+    plane = [pltpu.VMEM((RING * RING, rows + 8, width), jnp.bfloat16) for width in widths]
+    chosen = [pltpu.VMEM((8, RING, RING, SLOTS, width), jnp.bfloat16) for width in widths]
     own = pltpu.VMEM((rows + 8, model), jnp.bfloat16)
     dma = pltpu.SemaphoreType.DMA
     return pl.pallas_call(
@@ -369,8 +370,8 @@
         out_shape=(out, out, meta, meta, residual, residual, out),
         in_specs=[vmem_spec] * 10 + [any_spec] * 7,
         out_specs=(any_spec,) * 2 + (vmem_spec,) * 4 + (any_spec,),
-        scratch_shapes=plane * 2
-        + chosen * 2
+        scratch_shapes=plane
+        + chosen
         + [dma((2, 3, 16)), dma((2, 3)), dma((2,)), dma((2, 3)), dma((2, 3))]
         + [own, own, pltpu.VMEM((model, rows), jnp.bfloat16), pltpu.VMEM((rows, model), jnp.float32), pltpu.VMEM((3, 128, 128), jnp.float32)]
         + [pltpu.VMEM((8,) + block, jnp.bfloat16), dma((2,))]
@@ -387,14 +388,15 @@
     out_refs = (done_a, done_b)
     back = [scratch[0 + 3 * n : 3 + 3 * n] for n in range(batches)]
     rows = [scratch[6 + 3 * n : 9 + 3 * n] for n in range(batches)]
-    sums, got = scratch[12:15], [scratch[15 + 3 * n : 18 + 3 * n] for n in range(batches)]
+    sums = (scratch[12:15], scratch[12:15][::-1])
+    got = [scratch[15 + 3 * n : 18 + 3 * n] for n in range(batches)]
     kept = scratch[21]
     back_recv, back_send, own_sem, rows_recv, rows_send, sums_recv, sums_send = scratch[22:29]
     ids_ref, pool = scratch[29:31]
     held, (w_sem, x_sem, o_sem) = scratch[31:34], scratch[34:]
     tokens = y_refs[0].shape[0]
     barrier, greetings = greet()
-    for part, (_, _, order) in enumerate(PARTS):
+    for part, order in enumerate(ORDERS):
         for off2 in range(RING):
             ids_ref[part, off2] = row_ids(order, off2)
     pl.semaphore_wait(barrier, greetings)
@@ -403,23 +405,23 @@
     def hand_out(n):
         for part in range(3):
             for off2 in range(RING):
-                pltpu.make_async_copy(group_view(out_refs[n], part, 0, 0, off2), back[n][part].at[0, off2], own_sem.at[n, part]).start()
+                pltpu.make_async_copy(group_view(out_refs[n], n, part, 0, 0, off2), back[n][part].at[0, off2], own_sem.at[n, part]).start()
         for off2 in (2, 1, 3, 0):
             for i in (2, 3, 6, 7, 4, 5, 1):
                 off3, flip = PAIRS[i]
                 for part in range(3):
-                    s3 = PARTS[part][2][2]
-                    send(group_view(out_refs[n], part, off3, flip, off2), back[n][part].at[i, off2], back_send.at[n, part], back_recv.at[n, part, off2], peer(s3, -off3, flip)).start()
+                    s3 = ORDERS[part][2]
+                    send(group_view(out_refs[n], n, part, off3, flip, off2), back[n][part].at[i, off2], back_send.at[n, part], back_recv.at[n, part, off2], peer(s3, -off3, flip)).start()
 
     def turn(n, off2):
         for part in range(3):
-            s2 = PARTS[part][2][1]
+            s2 = ORDERS[part][1]
             drain(back[n][part].at[1:8, off2], back_recv.at[n, part, off2])
             if off2:
                 send(back[n][part].at[:, off2], rows[n][part].at[off2 - 1], rows_send.at[n, part], rows_recv.at[n, part, off2 - 1], peer(s2, -off2)).start()
 
     def weighted(n, part, off2, off1):
-        width = PARTS[part][1]
+        width = PARTS[n][part][1]
         meta = meta_refs[n][part, off1]
         dest = routing_ids(meta)
         gates = meta[:, 256:384].astype(jnp.float32)
@@ -440,12 +442,12 @@
         def flush():
             if late:
                 part = late.pop()
-                s1 = PARTS[part][2][0]
+                s1 = ORDERS[part][0]
                 for rows_half, off in ((slice(0, tokens // 2), -1), (slice(tokens // 2, tokens), 1)):
-                    send(sums[part].at[1, rows_half], got[n][part].at[2, rows_half], sums_send.at[part], sums_recv.at[n, part, 2], peer(s1, off)).start()
-
-        for part in range(3):
-            start, width, _ = PARTS[part]
+                    send(sums[n][part].at[1, rows_half], got[n][part].at[2, rows_half], sums_send.at[part], sums_recv.at[n, part, 2], peer(s1, off)).start()
+
+        for part in range(3):
+            start, width, _ = PARTS[n][part]
             if off2:
                 drain(rows[n][part].at[off2 - 1], rows_recv.at[n, part, off2 - 1])
             for off1 in (2, 1, 3, 0):
@@ -454,35 +456,35 @@
                     before = res_refs[n][:, start : start + width].astype(jnp.float32) if first else kept[:, start : start + width]
                     kept[:, start : start + width] = before + term
                 else:
-                    sums[part][off1 - 1] = term if first else sums[part][off1 - 1] + term
+                    sums[n][part][off1 - 1] = term if first else sums[n][part][off1 - 1] + term
                 flush()
                 if last and off1 == 2:
                     late.append(part)
 
     def pass_on(n):
         def out(part):
-            s1 = PARTS[part][2][0]
+            s1 = ORDERS[part][0]
             for off1, place in ((1, 0), (3, 1)):
-                send(sums[part].at[off1 - 1], got[n][part].at[place], sums_send.at[part], sums_recv.at[n, part, place], peer(s1, -off1)).start()
+                send(sums[n][part].at[off1 - 1], got[n][part].at[place], sums_send.at[part], sums_recv.at[n, part, place], peer(s1, -off1)).start()
 
         middle = tokens // 2
         for part in range(3):
             drain(got[n][part].at[2], sums_recv.at[n, part, 2])
-            sums[part][0, 0:middle] = sums[part][0, 0:middle] + got[n][part][2, 0:middle]
-            sums[part][2, middle:] = sums[part][2, middle:] + got[n][part][2, middle:]
+            sums[n][part][0, 0:middle] = sums[n][part][0, 0:middle] + got[n][part][2, 0:middle]
+            sums[n][part][2, middle:] = sums[n][part][2, middle:] + got[n][part][2, middle:]
             if part:
                 out(part - 1)
         out(2)
 
     def finish(n):
         for part in range(3):
-            start, width, _ = PARTS[part]
+            start, width, _ = PARTS[n][part]
             total = kept[:, start : start + width]
             for place in range(2):
                 drain(got[n][part].at[place], sums_recv.at[n, part, place])
                 total = total + got[n][part][place]
             y_refs[n][:, start : start + width] = total.astype(y_refs[n].dtype)
-            drain(sums[part], sums_send.at[part])
+            drain(sums[n][part], sums_send.at[part])
 
     hand_out(0)
     for copy in weight_copies:
@@ -528,7 +530,7 @@
     ffn = weights[0].shape[1]
     y = jax.ShapeDtypeStruct((tokens, model), jnp.bfloat16)
     any_spec, vmem_spec = pl.BlockSpec(memory_space=pl.ANY), pl.BlockSpec(memory_space=pltpu.VMEM)
-    widths = [width for _, width, _ in PARTS]
+    widths = [width for parts in PARTS for _, width, _ in parts]
     back = [pltpu.VMEM((8, RING, RING, SLOTS, width), jnp.bfloat16) for width in widths]
     rows = [pltpu.VMEM((RING - 1, 8, RING, SLOTS, width), jnp.bfloat16) for width in widths]
     sums = [pltpu.VMEM((RING - 1, tokens, width), jnp.float32) for width in widths]
@@ -538,7 +540,7 @@
         out_shape=(y, y, jax.ShapeDtypeStruct(x_b.shape, x_b.dtype)),
         in_specs=[any_spec] * 2 + [vmem_spec] * 4 + [any_spec] * 3,
         out_specs=(vmem_spec, vmem_spec, any_spec),
-        scratch_shapes=back * 2 + rows * 2 + sums * 3 + [pltpu.VMEM((tokens, model), jnp.float32)]
+        scratch_shapes=back + rows + sums[:3] + sums + [pltpu.VMEM((tokens, model), jnp.float32)]
         + [dma((2, 3, RING)), dma((2, 3)), dma((2, 3)), dma((2, 3, 3)), dma((2, 3)), dma((2, 3, 3)), dma((3,))]
         + [pltpu.VMEM((3, RING, 128, 128), jnp.float32), pltpu.VMEM((4,) + x_b.shape[1:], jnp.bfloat16)]
         + expert_scratch(model, ffn),
@@ -547,6 +549,15 @@
     )(done_a, x_b, *metas, *residuals, *weights)[:2]
 
 
+def hand_over_kernel(a_ref, b_ref, a_out, b_out):
+    a_out[...] = a_ref[...]
+    b_out[...] = b_ref[...]
+
+
+def hand_over(y_a, y_b):
+    return pl.pallas_call(hand_over_kernel, out_shape=tuple(jax.ShapeDtypeStruct(y.shape, y.dtype) for y in (y_a, y_b)), name="hand_over")(y_a, y_b)
+
+
 def solution(mesh):
     row_spec = P(("dp", "ep"), None)
     full_spec = P(None, None, None)
@@ -559,6 +570,6 @@
         attention_weights = [jnp.transpose(w, (1, 2, 0)) for w in (w_query, w_key, w_value)] + [w_out]
         routing = [(e.T, s.T, g.T) for e, s, g in ((experts_a, slots_a, gates_a), (experts_b, slots_b, gates_b))]
         _, x_b, meta_a, meta_b, res_a, res_b, done_a = dispatch((tokens_a, tokens_b), routing, (attn_gain, moe_gain), attention_weights, weights)
-        return bring_back(done_a, x_b, (meta_a, meta_b), (res_a, res_b), weights)
+        return hand_over(*bring_back(done_a, x_b, (meta_a, meta_b), (res_a, res_b), weights))
 
     return jax.shard_map(device_fn, mesh=mesh, in_specs=in_specs, out_specs=(row_spec, row_spec), check_vma=False)

time: 324 us -> 320 us (0.988)
  local copies, waits for them, and re-layouts: 3.76 us -> 0 us
    pallas_call x1, Pallas kernels: 154 us -> 150 us  [dispatch(): pl.pallas_call(dispatch_kernel, out_shape=(out, out, meta, meta, residual...]
    unnamed x2 -> x0, local copies, waits for them, and re-layouts: 3.76 us -> none
where the time goes in v4:
time: 320 us; the launch traced here: 319 us
  Pallas kernels  319 us (100%)
    pallas_call x1, Pallas kernels, bring_back(): pl.pallas_call(return_kernel, out_shape=(y, y, jax.ShapeDtypeStruct(x_b.s...  167 us
    pallas_call x1, Pallas kernels, dispatch(): pl.pallas_call(dispatch_kernel, out_shape=(out, out, meta, meta, residual...  150 us

profile of v4, /device:TPU:0, one launch (start us, length us, event | category | flops | bytes accessed | tf_op | source)
XLA Modules:
  0.0 319.2 jit_solution(17632361989055633149)
XLA Ops:
  0.6 149.8 %dispatch_rows.1 = (bf16[8,4,4,16,2048]{4,3,2,1,0:T(8,128)(2,1)}, bf16[8,4,4,16,2048]{4,3,2,1,0:T(8,128)(2,1)}, bf16[3,4,8,384]{3,2,1,0:T(8,128)(2,1)}, bf16[3,4...) custom-call(bf16[128,2048]{1,0:T(8,128)(2,1)} %refs_0_.1, ...), custom_call_target="tpu_custom_call" | custom-call | tf_op jit(solution)/shard_map/dispatch_rows/pallas_call | solution.py:368
  150.4 166.6 %return_rows.1 = (bf16[128,2048]{1,0:T(8,128)(2,1)}, bf16[128,2048]{1,0:T(8,128)(2,1)}, bf16[8,4,4,16,2048]{4,3,2,1,0:T(8,128)(2,1)}) custom-call(bf16[8,4,4,16,2048]{4,3,2,1,0:T(8,128)(2,1)} %get-tuple-element.10.refs_0_, bf16[8,4,4,16,2048]{4,3,2,1,0:T(8,128)(2,1)} %get-tuple-element.11.refs_1_, bf16[3,4,8,384]{3,2,1,0:T(8,128)(2,1)} %get-tuple-element.12.refs_2_, ...), custom_call_target="tpu_custom_call" | custom-call | tf_op jit(solution)/shard_map/return_rows/pallas_call | solution.py:538
  317.0 2.2 hand_over.1

commit v5 on v4

--- a/solution.py
+++ b/solution.py
@@ -92,6 +92,8 @@
         for w, w_ref in enumerate(w_refs):
             pltpu.make_async_copy(w_ref.at[i], pool.at[slot * 4 + w], sem.at[slot]).start()
 
+    if not last:
+        load(0, 0)
     normed_t[...] = rms_norm(x_ref[...].astype(jnp.float32), gain_ref).T.astype(jnp.bfloat16)
     total[...] = jnp.zeros_like(total)
     seen = lax.broadcasted_iota(jnp.int32, (tokens, tokens), 0) <= lax.broadcasted_iota(jnp.int32, (tokens, tokens), 1)
@@ -123,8 +125,6 @@
         between(i)
         return carry
 
-    if not last:
-        load(0, 0)
     lax.fori_loop(0, steps, step, 0)
 
 
@@ -300,10 +300,10 @@
             forward(0, True)
 
     attention(0, lambda i: None)
+    pl.semaphore_wait(barrier, greetings)
+    send_own(0)
     for part, order in enumerate(ORDERS):
         ids_ref[part] = row_ids(order, 0)
-    pl.semaphore_wait(barrier, greetings)
-    send_own(0)
     attention(1, under_b)
     weight_copies = load_weights(w_refs, held, w_sem)
     send_own(1)

time: 320 us -> 319 us (level)
  no operation moved by 1% of the time
where the time goes in v5:
time: 319 us
  Pallas kernels  318 us (100%)
    pallas_call x1, Pallas kernels, bring_back(): pl.pallas_call(return_kernel, out_shape=(y, y, jax.ShapeDtypeStruct(x_b.s...  167 us
    pallas_call x1, Pallas kernels, dispatch(): pl.pallas_call(dispatch_kernel, out_shape=(out, out, meta, meta, residual...  150 us

profile of v5, /device:TPU:0, one launch (start us, length us, event | category | flops | bytes accessed | tf_op | source)
XLA Modules:
  0.0 319.1 jit_solution(18322129743984969941)
XLA Ops:
  0.6 149.6 %dispatch_rows.1 = (bf16[8,4,4,16,2048]{4,3,2,1,0:T(8,128)(2,1)}, bf16[8,4,4,16,2048]{4,3,2,1,0:T(8,128)(2,1)}, bf16[3,4,8,384]{3,2,1,0:T(8,128)(2,1)}, bf16[3,4...) custom-call(bf16[128,2048]{1,0:T(8,128)(2,1)} %refs_0_.1, ...), custom_call_target="tpu_custom_call" | custom-call | tf_op jit(solution)/shard_map/dispatch_rows/pallas_call | solution.py:368
  150.3 166.6 %return_rows.1 = (bf16[128,2048]{1,0:T(8,128)(2,1)}, bf16[128,2048]{1,0:T(8,128)(2,1)}, bf16[8,4,4,16,2048]{4,3,2,1,0:T(8,128)(2,1)}) custom-call(bf16[8,4,4,16,2048]{4,3,2,1,0:T(8,128)(2,1)} %get-tuple-element.10.refs_0_, bf16[8,4,4,16,2048]{4,3,2,1,0:T(8,128)(2,1)} %get-tuple-element.11.refs_1_, bf16[3,4,8,384]{3,2,1,0:T(8,128)(2,1)} %get-tuple-element.12.refs_2_, ...), custom_call_target="tpu_custom_call" | custom-call | tf_op jit(solution)/shard_map/return_rows/pallas_call | solution.py:538
  316.9 2.2 hand_over.1
